TPU v7x, 32 devices: a whole 2x2x4 slice. The times are simulated.
32 devices in a mesh: facet: 4 (over y, core), team: 4 (over z), sub: 2 (over x).
Axes of the slice: x: 2, y: 2, z: 4, core: 2. Of those that a mesh axis runs over, the one named last changes fastest.
Arguments:
- facet_rows: bfloat16 [4, 2, 32, 4096], P('facet', None, 'team'), may hold values from -6 to 6
- sub_offsets: int32 [8, 2], replicated, may hold values from 0 to 4095
- facet_offsets: int32 [4, 2], replicated, may hold values from 0 to 4095
- aterm: bfloat16 [4, 2, 256, 256], P('facet'), may hold values from 0.29882812 to 3
- cells: int32 [4, 2, 4, 2, 256], P('facet', None, 'team'), may hold values from 0 to 1023
- observed: bfloat16 [4, 2, 4, 2, 256], P('facet', None, 'team'), may hold values from -6 to 6
- weights: bfloat16 [4, 2, 4, 256], P('facet', None, 'team'), may hold values from 0.29882812 to 3
- counts: int32 [4, 2, 4], replicated, may hold values from 1 to 256, as said below
Outputs:
- facet_update: float32 [4, 2, 32, 4096], P('facet', None, 'team', 'sub')
Inputs may be any that keep to these rules, and one draw needn't show every extreme that they name: Slots 0 to counts[a, b, t] - 1 are live. For every a and t one of the two subgrids with indices [a, 0] and [a, 1] has at most 64 live slots, and which of the two it is does not change with t.
All inputs are finite; a program needn't handle non-finite values.
Results may differ from a plain program's by a relative error of at most 0.019.
Values may be sent and summed in bfloat16 or wider, within the bound.
A program may use at most 64 MiB of HBM per device.

v0:
```python
import functools
import math

import jax
import jax.numpy as jnp
import ml_dtypes
import numpy as np
from jax import lax
from jax.experimental import pallas as pl
from jax.experimental.pallas import tpu as pltpu
from jax.sharding import PartitionSpec as P

M = 128
TWO_PI = 2.0 * math.pi
BF = jnp.bfloat16
F32 = jnp.float32
MESH = pl.DeviceIdType.MESH


def sincos(turns, period):
    shift = period.bit_length() - 3
    quad = (turns + (1 << (shift - 1))) >> shift
    t = (turns - (quad << shift)).astype(F32) * (TWO_PI / period)
    t2 = t * t
    s = t * (1.0 + t2 * (-1.0 / 6 + t2 * (1.0 / 120 + t2 * (-1.0 / 5040))))
    c = 1.0 + t2 * (-0.5 + t2 * (1.0 / 24 + t2 * (-1.0 / 720 + t2 * (1.0 / 40320))))
    odd = (quad & 1) != 0
    cos = jnp.where(odd, s, c)
    sin = jnp.where(odd, c, s)
    cos = jnp.where(((quad + 1) & 2) != 0, -cos, cos)
    sin = jnp.where((quad & 2) != 0, -sin, sin)
    return cos, sin


def mm(left, right):
    return jnp.dot(left, right, preferred_element_type=F32)


def mm_nt(left, right):
    return lax.dot_general(left, right, (((1,), (1,)), ((), ())), preferred_element_type=F32)


def cat(parts, axis):
    return jnp.concatenate(parts, axis)


def iota(shape, dim):
    return lax.broadcasted_iota(jnp.int32, shape, dim)


def body(
    dims,
    *refs,
):
    ins = refs[:12]
    out = refs[12]
    bufs = refs[13:25]
    (
    phi_c, phi_s, x_buf, spec_out, got1, fold_out, got2,
    send1, recv1, send2, recv2, in_sem,
    ) = refs[25:]
    sub_off, fac_off, counts, rows, aterm, cells, observed, weights, table, kk, kt, kb = bufs
    nf, nt, nb, length, size, rdev = dims
    rall = rdev * nt
    n = nf * nt
    slots = cells.shape[-1]
    period = 4 * size
    my_f = lax.axis_index("facet")
    my_t = lax.axis_index("team")
    my_b = lax.axis_index("sub")
    me = my_f * nt + my_t
    other = 1 - my_b

    def peer_of(k):
        peer = lax.rem(me + k, n)
        return peer, peer // nt, lax.rem(peer, nt)

    barrier = pltpu.get_barrier_semaphore()

    def greet(k, carry):
        _, pf, pt = peer_of(k)
        pl.semaphore_signal(
            barrier, inc=1, device_id={"facet": pf, "team": pt, "sub": my_b}, device_id_type=MESH
        )
        return carry

    lax.fori_loop(1, n, greet, 0)
    pl.semaphore_signal(
        barrier, inc=1, device_id={"facet": my_f, "team": my_t, "sub": other}, device_id_type=MESH
    )

    fetches = [pltpu.make_async_copy(ins[i], bufs[i], in_sem.at[i]) for i in range(12)]
    for i in (0, 3, 8, 1, 5, 10, 9, 4, 2, 6, 7, 11):
        fetches[i].start()
    fetches[0].wait()

    sub_row = iota((nb * nf, 1), 0)
    tune = jnp.zeros((nb * nf, 1), jnp.int32)
    for s in range(nf):
        tune = jnp.where(sub_row == s, sub_off[1, s * nb + my_b], tune)
        tune = jnp.where(sub_row == nf + s, sub_off[1, s * nb + other], tune)
    pc, ps = sincos(iota((nb * nf, length), 1) * tune, length)
    phi_c[...] = pc
    phi_s[...] = ps
    fetches[3].wait()
    re = rows[0, 0].astype(F32)
    im = rows[0, 1].astype(F32)
    for a in range(nf):
        c = phi_c[a : a + 1, :]
        s = phi_s[a : a + 1, :]
        x_buf[a] = re * c + im * s
        x_buf[nf + a] = im * c - re * s
    x = x_buf[...].reshape(2 * nf * rdev, length).astype(BF)
    fetches[8].wait()
    y = mm(x, table[...])
    h = nf * rdev
    spec = cat([y[:h, :M] - y[h:, M:], y[:h, M:] + y[h:, :M]], 1)
    spec_out[...] = spec.reshape(nf, rdev, 2 * M).astype(BF)

    pl.semaphore_wait(barrier, n)

    def copy1(k):
        peer, pf, pt = peer_of(k)
        return pltpu.make_async_remote_copy(
            src_ref=spec_out.at[pf],
            dst_ref=got1.at[me],
            send_sem=send1.at[k],
            recv_sem=recv1.at[me],
            device_id={"facet": pf, "team": pt, "sub": my_b},
            device_id_type=MESH,
        )

    def start1(k, carry):
        copy1(k).start()
        return carry

    lax.fori_loop(1, n, start1, 0)
    got1[me] = spec_out[my_f]

    for i in (1, 5, 10, 9, 4, 2, 6, 7, 11):
        fetches[i].wait()
    shift_u = sub_off[0, my_f * nb + my_b]
    step = length // rall
    scale_g = 1.0 / math.sqrt(rall * nf)
    lane = iota((1, n * rdev), 1)
    col_a = jnp.zeros((1, n * rdev), jnp.int32)
    row = iota((n * rdev, 1), 0)
    row_a = jnp.zeros((n * rdev, 1), jnp.int32)
    row_c = jnp.zeros((n * rdev, 1), jnp.int32)
    for f in range(nf):
        col_a = jnp.where(lane // rall == f, fac_off[0, f], col_a)
        row_a = jnp.where(row // rall == f, fac_off[0, f], row_a)
        row_c = jnp.where(row // rall == f, fac_off[1, f], row_c)
    p0 = iota((M, n * rdev), 0)
    gc, gs = sincos(p0 * col_a - (p0 + shift_u) * (lane % rall * step), length)
    gc = (gc * scale_g).astype(BF)
    gs = (gs * scale_g).astype(BF)
    a_mat = mm(kt[...], cat([cat([gc, gs], 1), cat([-gs, gc], 1)], 0)).astype(BF)
    p1 = iota((n * rdev, M), 1)
    hc, hs = sincos(p1 * row_a - (p1 + shift_u) * (row % rall * step), length)
    at = mm(cat([hc * scale_g, hs * scale_g], 1).astype(BF), kk[...])
    ah = cat([at[:, :size], -at[:, size:]], 1).astype(BF)
    ec, es = sincos(p1 * row_c, length)
    own_scale = math.sqrt(length / M) / size
    own_c, own_s = sincos(iota((rdev, M), 1) * fac_off[1, my_f], length)
    own_c = own_c * own_scale
    own_s = own_s * own_scale
    pair = cells[0, my_b, 0]
    index = iota((size, slots), 0)
    rc, rs = sincos(index * pair[0:1, :], period)
    rc = rc.astype(BF)
    rs = rs.astype(BF)
    cc, cs = sincos(index * pair[1:2, :], period)
    cc = cc.astype(BF)
    cs = cs.astype(BF)
    col_w = cat([cat([cc, -cs], 1), cat([cs, cc], 1)], 0)
    left = cat([rc, rs], 1)
    amap = aterm[0, my_b].astype(F32)
    amap = cat([amap, amap], 1)
    obs = observed[0, my_b, 0].astype(F32)
    live = iota((1, slots), 1) < counts[my_f, my_b, my_t]
    all_wt = weights[0, 0].astype(F32)
    own_wt = jnp.where(my_b == 0, all_wt[0:1, :], all_wt[1:2, :])
    wt = jnp.where(live, own_wt, 0.0)

    def take1(k, carry):
        peer, _, _ = peer_of(k)
        pltpu.make_async_copy(got1.at[peer], got1.at[peer], recv1.at[peer]).wait()
        return carry

    lax.fori_loop(1, n, take1, 0)
    sp = got1[...].astype(F32).reshape(n * rdev, 2 * M)
    sr = sp[:, :M]
    si = sp[:, M:]
    turned = cat([sr * ec - si * es, sr * es + si * ec], 1).astype(BF)
    t = mm(turned, kk[...]).astype(BF)
    tr = t[:, :size]
    ti = t[:, size:]
    image = mm(a_mat, cat([t, cat([-ti, tr], 1)], 0))
    weighted = (amap * image).astype(BF)
    z = mm(weighted, col_w)
    zr = z[:, :slots]
    zi = z[:, slots:]
    rcf = rc.astype(F32)
    rsf = rs.astype(F32)
    pred_re = jnp.sum(rcf * zr + rsf * zi, 0, keepdims=True) * (1.0 / size)
    pred_im = jnp.sum(rcf * zi - rsf * zr, 0, keepdims=True) * (1.0 / size)
    res_re = wt * (obs[0:1, :] - pred_re)
    res_im = wt * (obs[1:2, :] - pred_im)
    ccf = cc.astype(F32)
    csf = cs.astype(F32)
    s_re = (res_re * ccf - res_im * csf).astype(BF)
    s_im = (res_re * csf + res_im * ccf).astype(BF)
    grid = mm_nt(left, cat([cat([s_re, -s_im], 1), cat([s_im, s_re], 1)], 0))
    v = (amap * grid).astype(BF)
    u = mm(v, kb[...]).astype(BF)
    ur = u[:, :M]
    ui = u[:, M:]
    part = mm(ah, cat([u, cat([-ui, ur], 1)], 0))
    fold_out[...] = part.reshape(n, rdev, 2 * M).astype(BF)

    def copy2(k, far):
        peer, pf, pt = peer_of(k)
        return pltpu.make_async_remote_copy(
            src_ref=fold_out.at[peer],
            dst_ref=got2.at[far, me],
            send_sem=send2.at[far, k],
            recv_sem=recv2.at[far, me],
            device_id={"facet": pf, "team": pt, "sub": other if far else my_b},
            device_id_type=MESH,
        )

    def start2(k, carry):
        copy2(k, 1).start()
        copy2(k, 0).start()
        return carry

    copy2(0, 1).start()
    lax.fori_loop(1, n, start2, 0)
    got2[0, me] = fold_out[me]

    def take2(far):
        def step(k, carry):
            peer, _, _ = peer_of(k)
            slot = got2.at[far, peer]
            pltpu.make_async_copy(slot, slot, recv2.at[far, peer]).wait()
            return carry

        lax.fori_loop(1 - far, n, step, 0)
        parts = got2[far].astype(F32).reshape(nf, nt, rdev, 2 * M)
        folded = jnp.sum(parts, 1)
        fr = folded[:, :, :M]
        fi = folded[:, :, M:]
        oc = own_c[None]
        os_ = own_s[None]
        return cat([fr * oc + fi * os_, fi * oc - fr * os_], 2)

    half = length // nb
    base = pl.multiple_of(my_b * half, 128)
    back = table[pl.ds(base, half), :]

    def update(stack, first):
        stack = stack.reshape(nf * rdev, 2 * M)
        turned = cat([stack[:, M:], -stack[:, :M]], 1)
        pre = mm_nt(cat([stack, turned], 0).astype(BF), back)
        tot_re = tot_im = None
        for a in range(nf):
            c = phi_c[first + a : first + a + 1, pl.ds(base, half)]
            s = phi_s[first + a : first + a + 1, pl.ds(base, half)]
            pr = pre[a * rdev : (a + 1) * rdev]
            pi = pre[h + a * rdev : h + (a + 1) * rdev]
            add_re = pr * c - pi * s
            add_im = pi * c + pr * s
            tot_re = add_re if tot_re is None else tot_re + add_re
            tot_im = add_im if tot_im is None else tot_im + add_im
        return tot_re, tot_im

    own_re, own_im = update(take2(0), 0)
    oth_re, oth_im = update(take2(1), nf)
    out[0, 0] = own_re + oth_re
    out[0, 1] = own_im + oth_im

    def finish(k, carry):
        copy1(k).wait_send()
        copy2(k, 0).wait_send()
        copy2(k, 1).wait_send()
        return carry

    lax.fori_loop(1, n, finish, 0)
    copy2(0, 1).wait_send()


def tables(length, size):
    turn = np.arange(length)[:, None] * np.arange(M)[None, :] % length
    angle = turn * (TWO_PI / length)
    forward = np.concatenate([np.cos(angle), -np.sin(angle)], 1) / math.sqrt(length)
    angle = (np.arange(M)[:, None] * np.arange(size)[None, :] % size) * (TWO_PI / size)
    kc = np.cos(angle) / math.sqrt(M)
    ks = np.sin(angle) / math.sqrt(M)
    kk = np.block([[kc, ks], [-ks, kc]])
    kt = np.concatenate([kc.T, ks.T], 1)
    kb = np.block([[kc.T, -ks.T], [ks.T, kc.T]])
    return [np.asarray(v, np.float32).astype(ml_dtypes.bfloat16) for v in (forward, kk, kt, kb)]


def local(facet_rows, sub_offsets, facet_offsets, aterm, cells, observed, weights, counts):
    nf = lax.axis_size("facet")
    nt = lax.axis_size("team")
    nb = lax.axis_size("sub")
    rdev, length = facet_rows.shape[2:]
    size = aterm.shape[-1]
    n = nf * nt
    dims = (nf, nt, nb, length, size, rdev)
    consts = [jnp.asarray(v) for v in tables(length, size)]
    hbm = pl.BlockSpec(memory_space=pltpu.HBM)
    operands = [
        sub_offsets.T, facet_offsets.T, counts, facet_rows, aterm, cells, observed,
        weights.transpose(0, 2, 1, 3), *consts,
    ]
    dma = pltpu.SemaphoreType.DMA
    return pl.pallas_call(
        functools.partial(body, dims),
        out_shape=pltpu.VMEM((1, 2, rdev, length // nb), F32),
        in_specs=[hbm] * 12,
        out_specs=pl.BlockSpec(memory_space=pltpu.VMEM),
        scratch_shapes=[
            *[pltpu.SMEM(v.shape, v.dtype) for v in operands[:3]],
            *[pltpu.VMEM(v.shape, v.dtype) for v in operands[3:]],
            pltpu.VMEM((nb * nf, length), F32),
            pltpu.VMEM((nb * nf, length), F32),
            pltpu.VMEM((2 * nf, rdev, length), F32),
            pltpu.VMEM((nf, rdev, 2 * M), BF),
            pltpu.VMEM((n, rdev, 2 * M), BF),
            pltpu.VMEM((n, rdev, 2 * M), BF),
            pltpu.VMEM((nb, n, rdev, 2 * M), BF),
            dma((n,)), dma((n,)), dma((nb, n)), dma((nb, n)), dma((12,)),
        ],
        compiler_params=pltpu.CompilerParams(
            collective_id=0, has_side_effects=True
        ),
    )(*operands)


def solution(mesh):
    placed = (
        P("facet", None, "team", None),
        P(),
        P(),
        P("facet", None, None, None),
        P("facet", None, "team", None, None),
        P("facet", None, "team", None, None),
        P("facet", None, "team", None),
        P(),
    )
    return jax.shard_map(
        local,
        mesh=mesh,
        in_specs=placed,
        out_specs=P("facet", None, "team", "sub"),
        check_vma=False,
    )
```

profile of v0, /device:TPU:0, one launch (start us, length us, event | category | flops | bytes accessed | tf_op | source)
XLA Modules:
  0.0 19.5 jit_solution(12976392606953504264)
XLA Ops:
  0.0 18.9 %shard_map.118 = f32[1,2,8,2048]{3,2,1,0:T(8,128)S(1)} custom-call(s32[2,8]{1,0:T(2,128)} %bitcast.3, s32[2,4]{1,0:T(2,128)} %bitcast.4, s32[4,2,4]{2,1,0:T(2,128)} %refs_2_.1, bf16[1,2,8,4096]{3,2,1,0:T(8,128)(2,1)} %refs_3_.1, bf16[1,2,256,256]{3,2,1,0:T(8,128)(2,1)} %refs_4_.1, s32[1,2,1,2,256]{4,3,2,1,0:T(2,128)} %refs_5_.1, ...), custom_call_target="tpu_custom_call" | custom-call | tf_op jit(solution)/shard_map/pallas_call | solution.py:321
  18.9 0.7 %copy.14 = f32[1,2,8,2048]{3,2,1,0:T(8,128)} copy(f32[1,2,8,2048]{3,2,1,0:T(8,128)S(1)} %shard_map.118) | data formatting | bytes 262144
where the time goes:
time: 19.7 us; the launch traced here: 19.5 us
  Pallas kernels  18.9 us (96%)
  local copies, waits for them, and re-layouts  0.66 us (3%)
    pallas_call x1, Pallas kernels, local(): pl.pallas_call(functools.partial(body, dims), out_shape=pltpu.VMEM((1, 2,...  18.9 us
    unnamed x1, local copies, waits for them, and re-layouts  0.66 us

commit v1 on v0

v1 whole, which is shorter than its diff:
```python
import functools
import math

import jax
import jax.numpy as jnp
import ml_dtypes
import numpy as np
from jax import lax
from jax.experimental import pallas as pl
from jax.experimental.pallas import tpu as pltpu
from jax.sharding import PartitionSpec as P

M = 128
LANES = 128
FINE = 16
TWO_PI = 2.0 * math.pi
BF = jnp.bfloat16
F32 = jnp.float32
MESH = pl.DeviceIdType.MESH


def sincos(turns, period):
    shift = period.bit_length() - 3
    quad = (turns + (1 << (shift - 1))) >> shift
    t = (turns - (quad << shift)).astype(F32) * (TWO_PI / period)
    t2 = t * t
    s = t * (1.0 + t2 * (-1.0 / 6 + t2 * (1.0 / 120 + t2 * (-1.0 / 5040))))
    c = 1.0 + t2 * (-0.5 + t2 * (1.0 / 24 + t2 * (-1.0 / 720 + t2 * (1.0 / 40320))))
    odd = (quad & 1) != 0
    cos = jnp.where(odd, s, c)
    sin = jnp.where(odd, c, s)
    cos = jnp.where(((quad + 1) & 2) != 0, -cos, cos)
    sin = jnp.where((quad & 2) != 0, -sin, sin)
    return cos, sin


def mm(left, right):
    return jnp.dot(left, right, preferred_element_type=F32)


def mm_nt(left, right):
    return lax.dot_general(left, right, (((1,), (1,)), ((), ())), preferred_element_type=F32)


def cat(parts, axis):
    return jnp.concatenate(parts, axis)


def iota(shape, dim):
    return lax.broadcasted_iota(jnp.int32, shape, dim)


def body(dims, *refs):
    (sub_hbm, fac_hbm, cnt_hbm, rows_hbm, aterm_hbm, cells_hbm, obs_hbm, wt_hbm, kk_hbm, kt_hbm, kb_hbm) = refs[:11]
    out_hbm = refs[11]
    (
        sub_off, fac_off, counts, rows, aterm, cells, observed, weights, kk, kt, kb,
        spec_out, got1, slot_out, got_x, fold_out, got2, out_buf,
        tw1, tw2, wt_near, wt_far, fine, col_w, row_c, row_s, res,
        send1, recv1, send_x, recv_x, send2, recv2, in_sem, out_sem,
    ) = refs[12:]
    nf, nt, nb, length, size, rdev = dims
    rall = rdev * nt
    n = nf * nt
    slots = cells.shape[-1]
    period = 4 * size
    tiles = length // LANES
    my_f = lax.axis_index("facet")
    my_t = lax.axis_index("team")
    my_b = lax.axis_index("sub")
    me = my_f * nt + my_t
    other = 1 - my_b

    fetches = [
        pltpu.make_async_copy(sub_hbm, sub_off, in_sem.at[0]),
        pltpu.make_async_copy(rows_hbm, rows, in_sem.at[1]),
        pltpu.make_async_copy(fac_hbm, fac_off, in_sem.at[2]),
        pltpu.make_async_copy(cnt_hbm, counts, in_sem.at[3]),
        pltpu.make_async_copy(cells_hbm.at[0, my_b, 0], cells, in_sem.at[4]),
        pltpu.make_async_copy(obs_hbm.at[0, my_b, 0], observed, in_sem.at[5]),
        pltpu.make_async_copy(wt_hbm, weights, in_sem.at[6]),
        pltpu.make_async_copy(kt_hbm, kt, in_sem.at[7]),
        pltpu.make_async_copy(kk_hbm, kk, in_sem.at[8]),
        pltpu.make_async_copy(aterm_hbm.at[0, my_b], aterm, in_sem.at[9]),
        pltpu.make_async_copy(kb_hbm, kb, in_sem.at[10]),
    ]
    for fetch in fetches:
        fetch.start()

    barrier = pltpu.get_barrier_semaphore()

    def peer_of(q):
        f = lax.rem(my_f + lax.rem(q + 1, nf), nf)
        t = lax.rem(my_t + lax.rem(q // nf + 1, nt), nt)
        return f, t

    def greet(q, carry):
        f, t = peer_of(q)
        pl.semaphore_signal(
            barrier, inc=1, device_id={"facet": f, "team": t, "sub": my_b}, device_id_type=MESH
        )
        return carry

    lax.fori_loop(0, n - 1, greet, 0)
    for f in range(nf):
        pl.semaphore_signal(
            barrier, inc=1, device_id={"facet": f, "team": my_t, "sub": other}, device_id_type=MESH
        )

    base_c, base_s = sincos(iota((M, LANES), 0) * iota((M, LANES), 1), length)
    lane_row = iota((1, LANES), 1)

    fetches[0].wait()

    def column_weights(shift_v):
        pc, ps = sincos(lane_row * shift_v, length)
        c = (base_c * pc - base_s * ps).astype(BF)
        s = (base_s * pc + base_c * ps).astype(BF)
        return cat([cat([c, s], 1), cat([-s, c], 1)], 0)

    scale = 1.0 / math.sqrt(length)
    for a in range(nf):
        shift_v = sub_off[1, a * nb + my_b]
        wt_near[a] = column_weights(shift_v)
        c, s = sincos(iota((tiles, M), 0) * (iota((tiles, M), 1) + shift_v), tiles)
        tw1[a, 0] = c * scale
        tw1[a, 1] = s * scale
    fetches[1].wait()
    x = [
        cat([rows[0, c, :, k * LANES : (k + 1) * LANES].astype(F32) for k in range(tiles)], 0)
        for c in range(2)
    ]
    x = cat(x, 1).astype(BF)
    for a in range(nf):
        y = mm_nt(x, wt_near[a])
        acc = [None] * 4
        for k in range(tiles):
            yr = y[k * rdev : (k + 1) * rdev, :M]
            yi = y[k * rdev : (k + 1) * rdev, M:]
            c = tw1[a, 0, k : k + 1, :]
            s = tw1[a, 1, k : k + 1, :]
            q = 2 * (k % 2)
            add_re = yr * c + yi * s
            add_im = yi * c - yr * s
            acc[q] = add_re if acc[q] is None else acc[q] + add_re
            acc[q + 1] = add_im if acc[q + 1] is None else acc[q + 1] + add_im
        spec_out[a] = cat([acc[0] + acc[2], acc[1] + acc[3]], 1).astype(BF)

    for i in (2, 3, 4, 5, 6):
        fetches[i].wait()
    live = iota((1, slots), 1) < counts[my_f, my_b, my_t]
    all_wt = weights[0, 0].astype(F32)
    own_wt = jnp.where(my_b == 0, all_wt[0:1, :], all_wt[1:2, :])
    own_wt = jnp.where(live, own_wt, 0.0)
    packed = cat(
        [cells[...].astype(F32), observed[...].astype(F32), own_wt, jnp.zeros((3, slots), F32)], 0
    )
    slot_out[...] = packed
    got_x[my_t] = packed

    pl.semaphore_wait(barrier, n - 1 + nf)

    def copy_x(k):
        return pltpu.make_async_remote_copy(
            src_ref=slot_out,
            dst_ref=got_x.at[my_t],
            send_sem=send_x,
            recv_sem=recv_x.at[my_t],
            device_id={"facet": my_f, "team": lax.rem(my_t + k, nt), "sub": my_b},
            device_id_type=MESH,
        )

    def copy1(q):
        f, t = peer_of(q)
        return pltpu.make_async_remote_copy(
            src_ref=spec_out.at[f],
            dst_ref=got1.at[me],
            send_sem=send1,
            recv_sem=recv1,
            device_id={"facet": f, "team": t, "sub": my_b},
            device_id_type=MESH,
        )

    for k in range(1, nt):
        copy_x(k).start()

    def start1(q, carry):
        copy1(q).start()
        return carry

    lax.fori_loop(0, n - 1, start1, 0)
    got1[me] = spec_out[my_f]

    for i in (7, 8, 9, 10):
        fetches[i].wait()
    shift_u = sub_off[0, my_f * nb + my_b]
    step = length // rall
    scale_g = 1.0 / math.sqrt(rall * nf)
    lane = iota((1, n * rdev), 1)
    col_a = jnp.zeros((1, n * rdev), jnp.int32)
    row = iota((n * rdev, 1), 0)
    row_cc = jnp.zeros((n * rdev, 1), jnp.int32)
    row2 = iota((nf * rdev, 1), 0)
    row_a = jnp.zeros((nf * rdev, 1), jnp.int32)
    for f in range(nf):
        col_a = jnp.where(lane // rall == f, fac_off[0, f], col_a)
        row_cc = jnp.where(row // rall == f, fac_off[1, f], row_cc)
        row_a = jnp.where(row2 // rdev == f, fac_off[0, f], row_a)
    p0 = iota((M, n * rdev), 0)
    gc, gs = sincos(p0 * col_a - (p0 + shift_u) * (lane % rall * step), length)
    gc = (gc * scale_g).astype(BF)
    gs = (gs * scale_g).astype(BF)
    a_mat = mm(kt[...], cat([cat([gc, gs], 1), cat([-gs, gc], 1)], 0)).astype(BF)
    p1 = iota((nf * rdev, M), 1)
    hc, hs = sincos(p1 * row_a - (p1 + shift_u) * ((row2 % rdev + my_t * rdev) * step), length)
    at = mm(cat([hc * scale_g, hs * scale_g], 1).astype(BF), kk[...])
    ah = cat([at[:, :size], -at[:, size:]], 1).astype(BF)
    ec, es = sincos(iota((n * rdev, M), 1) * row_cc, length)

    half = tiles // nb
    scale_b = 1.0 / (math.sqrt(M) * size)
    tile_no = iota((half, M), 0) + my_b * half
    for far in range(2):
        for a in range(nf):
            shift_v = sub_off[1, a * nb + (other if far else my_b)]
            if far:
                wt_far[a] = column_weights(shift_v)
            m_no = iota((half, M), 1)
            c, s = sincos((m_no + shift_v) * (tile_no * LANES) - m_no * fac_off[1, my_f], length)
            tw2[far, a, 0] = c * scale_b
            tw2[far, a, 1] = s * scale_b

    fine_no = iota((FINE, slots), 0)
    coarse = size // FINE
    coarse_no = iota((coarse, slots), 0) * FINE
    for k in range(nt):
        src = lax.rem(my_t + k, nt)
        if k:
            pltpu.make_async_copy(got_x.at[src], got_x.at[src], recv_x.at[src]).wait()
        pos = got_x[src, 0:2, :].astype(jnp.int32)
        for axis in range(2):
            lo_c, lo_s = sincos(fine_no * pos[axis : axis + 1, :], period)
            hi_c, hi_s = sincos(coarse_no * pos[axis : axis + 1, :], period)
            fine[0] = hi_c
            fine[1] = hi_s
            for q in range(coarse):
                c1 = fine[0, q : q + 1, :]
                s1 = fine[1, q : q + 1, :]
                c = c1 * lo_c - s1 * lo_s
                s = s1 * lo_c + c1 * lo_s
                rng = slice(q * FINE, (q + 1) * FINE)
                if axis == 0:
                    row_c[k, rng, :] = c
                    row_s[k, rng, :] = s
                else:
                    cb = c.astype(BF)
                    sb = s.astype(BF)
                    low = slice(size + q * FINE, size + (q + 1) * FINE)
                    col_w[k, rng, :slots] = cb
                    col_w[k, rng, slots:] = -sb
                    col_w[k, low, :slots] = sb
                    col_w[k, low, slots:] = cb
    amap = aterm[...].astype(F32)
    amap = cat([amap, amap], 1)

    done = got1.at[pl.ds(0, n - 1)]
    pltpu.make_async_copy(done, done, recv1).wait()
    sp = got1[...].astype(F32).reshape(n * rdev, 2 * M)
    sr = sp[:, :M]
    si = sp[:, M:]
    turned = cat([sr * ec - si * es, sr * es + si * ec], 1).astype(BF)
    t = mm(turned, kk[...]).astype(BF)
    tr = t[:, :size]
    ti = t[:, size:]
    image = mm(a_mat, cat([t, cat([-ti, tr], 1)], 0))
    weighted = (amap * image).astype(BF)
    grid = None
    for k in range(nt):
        src = lax.rem(my_t + k, nt)
        z = mm(weighted, col_w[k])
        zr = z[:, :slots]
        zi = z[:, slots:]
        rc = row_c[k]
        rs = row_s[k]
        pred_re = jnp.sum(rc * zr + rs * zi, 0, keepdims=True) * (1.0 / size)
        pred_im = jnp.sum(rc * zi - rs * zr, 0, keepdims=True) * (1.0 / size)
        info = got_x[src]
        res_re = info[4:5, :] * (info[2:3, :] - pred_re)
        res_im = info[4:5, :] * (info[3:4, :] - pred_im)
        res[k, 0:1, :] = res_re
        res[k, 1:2, :] = res_im
    for k in range(nt):
        rc = row_c[k]
        rs = row_s[k]
        res_re = res[k, 0:1, :]
        res_im = res[k, 1:2, :]
        left = cat([rc * res_re - rs * res_im, rc * res_im + rs * res_re], 1).astype(BF)
        part = mm_nt(left, col_w[k])
        grid = part if grid is None else grid + part
    v = (amap * grid).astype(BF)
    u = mm(v, kb[...]).astype(BF)
    ur = u[:, :M]
    ui = u[:, M:]
    part = mm(ah, cat([u, cat([-ui, ur], 1)], 0))
    fold_out[...] = part.reshape(nf, rdev, 2 * M).astype(BF)


    def copy2(k, far):
        f = lax.rem(my_f + k, nf)
        return pltpu.make_async_remote_copy(
            src_ref=fold_out.at[f],
            dst_ref=got2.at[far, my_f],
            send_sem=send2,
            recv_sem=recv2.at[far],
            device_id={"facet": f, "team": my_t, "sub": other if far else my_b},
            device_id_type=MESH,
        )

    for k in range(1, nf + 1):
        copy2(k % nf, 1).start()
    for k in range(1, nf):
        copy2(k, 0).start()
    got2[0, my_f] = fold_out[my_f]

    def update(far):
        left = []
        for a in range(nf):
            g = got2[far, a].astype(F32)
            gr = g[:, :M]
            gi = g[:, M:]
            parts = []
            for k in range(half):
                c = tw2[far, a, 0, k : k + 1, :]
                s = tw2[far, a, 1, k : k + 1, :]
                parts.append(cat([gr * c - gi * s, gr * s + gi * c], 1))
            left.append(cat(parts, 0).astype(BF))
        wts = wt_far if far else wt_near
        total = None
        for a in range(nf):
            y = mm(left[a], wts[a])
            total = y if total is None else total + y
        return total

    done = got2.at[0, pl.ds(0, nf - 1)]
    pltpu.make_async_copy(done, done, recv2.at[0]).wait()
    near = update(0)
    done = got2.at[1]
    pltpu.make_async_copy(done, done, recv2.at[1]).wait()
    total = near + update(1)
    for k in range(half):
        rng = slice(k * rdev, (k + 1) * rdev)
        lanes = slice(k * LANES, (k + 1) * LANES)
        out_buf[0, 0, :, lanes] = total[rng, :LANES]
        out_buf[0, 1, :, lanes] = total[rng, LANES:]
    write = pltpu.make_async_copy(out_buf, out_hbm, out_sem)
    write.start()
    for k in range(1, nt):
        copy_x(k).wait_send()
    sent = got1.at[pl.ds(0, n - 1)]
    pltpu.make_async_copy(sent, sent, send1).wait()
    sent = got1.at[pl.ds(0, 2 * nf - 1)]
    pltpu.make_async_copy(sent, sent, send2).wait()
    write.wait()


def tables(size):
    angle = (np.arange(M)[:, None] * np.arange(size)[None, :] % size) * (TWO_PI / size)
    kc = np.cos(angle) / math.sqrt(M)
    ks = np.sin(angle) / math.sqrt(M)
    kk = np.block([[kc, ks], [-ks, kc]])
    kt = np.concatenate([kc.T, ks.T], 1)
    kb = np.block([[kc.T, -ks.T], [ks.T, kc.T]])
    return [np.asarray(v, np.float32).astype(ml_dtypes.bfloat16) for v in (kk, kt, kb)]


def local(facet_rows, sub_offsets, facet_offsets, aterm, cells, observed, weights, counts):
    nf = lax.axis_size("facet")
    nt = lax.axis_size("team")
    nb = lax.axis_size("sub")
    rdev, length = facet_rows.shape[2:]
    size = aterm.shape[-1]
    slots = cells.shape[-1]
    n = nf * nt
    tiles = length // LANES
    dims = (nf, nt, nb, length, size, rdev)
    consts = [jnp.asarray(v) for v in tables(size)]
    hbm = pl.BlockSpec(memory_space=pltpu.HBM)
    operands = [
        sub_offsets.T, facet_offsets.T, counts, facet_rows, aterm, cells, observed,
        weights.transpose(0, 2, 1, 3), *consts,
    ]
    dma = pltpu.SemaphoreType.DMA
    vmem = pltpu.VMEM
    return pl.pallas_call(
        functools.partial(body, dims),
        out_shape=jax.ShapeDtypeStruct((1, 2, rdev, length // nb), F32),
        in_specs=[hbm] * 11,
        out_specs=hbm,
        scratch_shapes=[
            *[pltpu.SMEM(v.shape, v.dtype) for v in operands[:3]],
            vmem(facet_rows.shape, BF),
            vmem((size, size), BF),
            vmem((2, slots), jnp.int32),
            vmem((2, slots), BF),
            *[vmem(v.shape, v.dtype) for v in operands[7:]],
            vmem((nf, rdev, 2 * M), BF),
            vmem((n, rdev, 2 * M), BF),
            vmem((8, slots), F32),
            vmem((nt, 8, slots), F32),
            vmem((nf, rdev, 2 * M), BF),
            vmem((nb, nf, rdev, 2 * M), BF),
            vmem((1, 2, rdev, length // nb), F32),
            vmem((nf, 2, tiles, M), F32),
            vmem((nb, nf, 2, tiles // nb, M), F32),
            vmem((nf, 2 * M, 2 * LANES), BF),
            vmem((nf, 2 * M, 2 * LANES), BF),
            vmem((2, size // FINE, slots), F32),
            vmem((nt, 2 * size, 2 * slots), BF),
            vmem((nt, size, slots), F32),
            vmem((nt, size, slots), F32),
            vmem((nt, 8, slots), F32),
            dma, dma, dma, dma((nt,)), dma, dma((nb,)), dma((11,)), dma,
        ],
        compiler_params=pltpu.CompilerParams(
            collective_id=0, has_side_effects=True
        ),
    )(*operands)


def solution(mesh):
    placed = (
        P("facet", None, "team", None),
        P(),
        P(),
        P("facet", None, None, None),
        P("facet", None, "team", None, None),
        P("facet", None, "team", None, None),
        P("facet", None, "team", None),
        P(),
    )
    return jax.shard_map(
        local,
        mesh=mesh,
        in_specs=placed,
        out_specs=P("facet", None, "team", "sub"),
        check_vma=False,
    )
```

time: 19.7 us -> 18.4 us (0.934)
  Pallas kernels: 18.9 us -> 16.7 us
  local copies, waits for them, and re-layouts: 0.66 us -> 1.57 us
    pallas_call x1, Pallas kernels: 18.9 us -> 16.7 us  [local(): pl.pallas_call(functools.partial(body, dims), out_shape=jax.ShapeDtypeStr...]
    unnamed x1, local copies, waits for them, and re-layouts: 0.66 us -> 1.57 us
where the time goes in v1:
time: 18.4 us; the launch traced here: 18.3 us
  Pallas kernels  16.7 us (91%)
  local copies, waits for them, and re-layouts  1.57 us (9%)
    pallas_call x1, Pallas kernels, local(): pl.pallas_call(functools.partial(body, dims), out_shape=jax.ShapeDtypeStr...  16.7 us
    unnamed x1, local copies, waits for them, and re-layouts  1.57 us

profile of v1, /device:TPU:0, one launch (start us, length us, event | category | flops | bytes accessed | tf_op | source)
XLA Modules:
  0.0 18.3 jit_solution(7527530746387763341)
XLA Ops:
  0.0 16.7 %shard_map.109 = f32[1,2,8,2048]{3,2,1,0:T(8,128)} custom-call(s32[2,8]{1,0:T(2,128)} %bitcast.3, s32[2,4]{1,0:T(2,128)} %bitcast.4, s32[4,2,4]{2,1,0:T(2,128)} %refs_2_.1, bf16[1,2,8,4096]{3,2,1,0:T(8,128)(2,1)} %refs_3_.1, bf16[1,2,256,256]{3,2,1,0:T(8,128)(2,1)} %refs_4_.1, s32[1,2,1,2,256]{4,3,2,1,0:T(2,128)} %refs_5_.1, ...), custom_call_target="tpu_custom_call" | custom-call | tf_op jit(solution)/shard_map/pallas_call | solution.py:394
  16.7 1.6 %copy.13 = f32[1,2,8,2048]{3,2,1,0:T(8,128)} copy(f32[1,2,8,2048]{3,2,1,0:T(8,128)} %shard_map.109) | data formatting | bytes 262144

commit v2 on v1

--- a/solution.py
+++ b/solution.py
@@ -13,6 +13,7 @@
 M = 128
 LANES = 128
 FINE = 16
+HALF_BITS = 5
 TWO_PI = 2.0 * math.pi
 BF = jnp.bfloat16
 F32 = jnp.float32
@@ -52,12 +53,12 @@
 
 def body(dims, *refs):
     (sub_hbm, fac_hbm, cnt_hbm, rows_hbm, aterm_hbm, cells_hbm, obs_hbm, wt_hbm, kk_hbm, kt_hbm, kb_hbm) = refs[:11]
-    out_hbm = refs[11]
+    out = refs[11]
     (
         sub_off, fac_off, counts, rows, aterm, cells, observed, weights, kk, kt, kb,
-        spec_out, got1, slot_out, got_x, fold_out, got2, out_buf,
+        spec_out, got1, slot_out, got_x, fold_out, got2,
         tw1, tw2, wt_near, wt_far, fine, col_w, row_c, row_s, res,
-        send1, recv1, send_x, recv_x, send2, recv2, in_sem, out_sem,
+        send1, recv1, send_x, recv_x, send2, recv2, in_sem,
     ) = refs[12:]
     nf, nt, nb, length, size, rdev = dims
     rall = rdev * nt
@@ -152,9 +153,14 @@
     all_wt = weights[0, 0].astype(F32)
     own_wt = jnp.where(my_b == 0, all_wt[0:1, :], all_wt[1:2, :])
     own_wt = jnp.where(live, own_wt, 0.0)
+    place = cells[...]
     packed = cat(
-        [cells[...].astype(F32), observed[...].astype(F32), own_wt, jnp.zeros((3, slots), F32)], 0
-    )
+        [
+            (place >> HALF_BITS).astype(F32), (place & ((1 << HALF_BITS) - 1)).astype(F32),
+            observed[...].astype(F32), own_wt, own_wt,
+        ],
+        0,
+    ).astype(BF)
     slot_out[...] = packed
     got_x[my_t] = packed
 
@@ -170,8 +176,9 @@
             device_id_type=MESH,
         )
 
-    def copy1(q):
-        f, t = peer_of(q)
+    def copy1(df, dt):
+        f = lax.rem(my_f + df, nf)
+        t = lax.rem(my_t + dt, nt)
         return pltpu.make_async_remote_copy(
             src_ref=spec_out.at[f],
             dst_ref=got1.at[me],
@@ -181,14 +188,13 @@
             device_id_type=MESH,
         )
 
-    for k in range(1, nt):
-        copy_x(k).start()
-
-    def start1(q, carry):
-        copy1(q).start()
-        return carry
-
-    lax.fori_loop(0, n - 1, start1, 0)
+    for dt in range(1, nt + 1):
+        if dt < nt:
+            copy_x(dt).start()
+        for df in range(nf):
+            df = (df + nf // 2) % nf
+            if df or dt < nt:
+                copy1(df, dt % nt).start()
     got1[me] = spec_out[my_f]
 
     for i in (7, 8, 9, 10):
@@ -237,7 +243,8 @@
         src = lax.rem(my_t + k, nt)
         if k:
             pltpu.make_async_copy(got_x.at[src], got_x.at[src], recv_x.at[src]).wait()
-        pos = got_x[src, 0:2, :].astype(jnp.int32)
+        pos = got_x[src].astype(F32)[0:4, :].astype(jnp.int32)
+        pos = (pos[0:2, :] << HALF_BITS) + pos[2:4, :]
         for axis in range(2):
             lo_c, lo_s = sincos(fine_no * pos[axis : axis + 1, :], period)
             hi_c, hi_s = sincos(coarse_no * pos[axis : axis + 1, :], period)
@@ -284,9 +291,9 @@
         rs = row_s[k]
         pred_re = jnp.sum(rc * zr + rs * zi, 0, keepdims=True) * (1.0 / size)
         pred_im = jnp.sum(rc * zi - rs * zr, 0, keepdims=True) * (1.0 / size)
-        info = got_x[src]
-        res_re = info[4:5, :] * (info[2:3, :] - pred_re)
-        res_im = info[4:5, :] * (info[3:4, :] - pred_im)
+        info = got_x[src].astype(F32)
+        res_re = info[6:7, :] * (info[4:5, :] - pred_re)
+        res_im = info[6:7, :] * (info[5:6, :] - pred_im)
         res[k, 0:1, :] = res_re
         res[k, 1:2, :] = res_im
     for k in range(nt):
@@ -350,17 +357,14 @@
     for k in range(half):
         rng = slice(k * rdev, (k + 1) * rdev)
         lanes = slice(k * LANES, (k + 1) * LANES)
-        out_buf[0, 0, :, lanes] = total[rng, :LANES]
-        out_buf[0, 1, :, lanes] = total[rng, LANES:]
-    write = pltpu.make_async_copy(out_buf, out_hbm, out_sem)
-    write.start()
+        out[0, 0, :, lanes] = total[rng, :LANES]
+        out[0, 1, :, lanes] = total[rng, LANES:]
     for k in range(1, nt):
         copy_x(k).wait_send()
     sent = got1.at[pl.ds(0, n - 1)]
     pltpu.make_async_copy(sent, sent, send1).wait()
     sent = got1.at[pl.ds(0, 2 * nf - 1)]
     pltpu.make_async_copy(sent, sent, send2).wait()
-    write.wait()
 
 
 def tables(size):
@@ -393,9 +397,9 @@
     vmem = pltpu.VMEM
     return pl.pallas_call(
         functools.partial(body, dims),
-        out_shape=jax.ShapeDtypeStruct((1, 2, rdev, length // nb), F32),
+        out_shape=pltpu.VMEM((1, 2, rdev, length // nb), F32),
         in_specs=[hbm] * 11,
-        out_specs=hbm,
+        out_specs=pl.BlockSpec(memory_space=pltpu.VMEM),
         scratch_shapes=[
             *[pltpu.SMEM(v.shape, v.dtype) for v in operands[:3]],
             vmem(facet_rows.shape, BF),
@@ -405,11 +409,10 @@
             *[vmem(v.shape, v.dtype) for v in operands[7:]],
             vmem((nf, rdev, 2 * M), BF),
             vmem((n, rdev, 2 * M), BF),
-            vmem((8, slots), F32),
-            vmem((nt, 8, slots), F32),
+            vmem((8, slots), BF),
+            vmem((nt, 8, slots), BF),
             vmem((nf, rdev, 2 * M), BF),
             vmem((nb, nf, rdev, 2 * M), BF),
-            vmem((1, 2, rdev, length // nb), F32),
             vmem((nf, 2, tiles, M), F32),
             vmem((nb, nf, 2, tiles // nb, M), F32),
             vmem((nf, 2 * M, 2 * LANES), BF),
@@ -419,7 +422,7 @@
             vmem((nt, size, slots), F32),
             vmem((nt, size, slots), F32),
             vmem((nt, 8, slots), F32),
-            dma, dma, dma, dma((nt,)), dma, dma((nb,)), dma((11,)), dma,
+            dma, dma, dma, dma((nt,)), dma, dma((nb,)), dma((11,)),
         ],
         compiler_params=pltpu.CompilerParams(
             collective_id=0, has_side_effects=True

time: 18.4 us -> 16.4 us (0.89)
  Pallas kernels: 16.7 us -> 15.5 us
  local copies, waits for them, and re-layouts: 1.57 us -> 0.66 us
    pallas_call x1, Pallas kernels: 16.7 us -> 15.5 us  [local(): pl.pallas_call(functools.partial(body, dims), out_shape=pltpu.VMEM((1, 2,...]
    unnamed x1, local copies, waits for them, and re-layouts: 1.57 us -> 0.66 us
where the time goes in v2:
time: 16.4 us; the launch traced here: 16.2 us
  Pallas kernels  15.5 us (95%)
  local copies, waits for them, and re-layouts  0.66 us (4%)
    pallas_call x1, Pallas kernels, local(): pl.pallas_call(functools.partial(body, dims), out_shape=pltpu.VMEM((1, 2,...  15.5 us
    unnamed x1, local copies, waits for them, and re-layouts  0.66 us

profile of v2, /device:TPU:0, one launch (start us, length us, event | category | flops | bytes accessed | tf_op | source)
XLA Modules:
  0.0 16.2 jit_solution(18191855233638782009)
XLA Ops:
  0.0 15.5 %shard_map.109 = f32[1,2,8,2048]{3,2,1,0:T(8,128)S(1)} custom-call(s32[2,8]{1,0:T(2,128)} %bitcast.3, s32[2,4]{1,0:T(2,128)} %bitcast.4, s32[4,2,4]{2,1,0:T(2,128)} %refs_2_.1, bf16[1,2,8,4096]{3,2,1,0:T(8,128)(2,1)} %refs_3_.1, bf16[1,2,256,256]{3,2,1,0:T(8,128)(2,1)} %refs_4_.1, s32[1,2,1,2,256]{4,3,2,1,0:T(2,128)} %refs_5_.1, ...), custom_call_target="tpu_custom_call" | custom-call | tf_op jit(solution)/shard_map/pallas_call | solution.py:398
  15.5 0.7 %copy.13 = f32[1,2,8,2048]{3,2,1,0:T(8,128)} copy(f32[1,2,8,2048]{3,2,1,0:T(8,128)S(1)} %shard_map.109) | data formatting | bytes 262144

commit v3 on v2

--- a/solution.py
+++ b/solution.py
@@ -89,29 +89,34 @@
         fetch.start()
 
     barrier = pltpu.get_barrier_semaphore()
-
-    def peer_of(q):
-        f = lax.rem(my_f + lax.rem(q + 1, nf), nf)
-        t = lax.rem(my_t + lax.rem(q // nf + 1, nt), nt)
-        return f, t
-
-    def greet(q, carry):
-        f, t = peer_of(q)
+    nc = 2 - nf % 2
+    ny = nf // nc
+    order = [(k // nc + ny // 2) % ny * nc + k % nc for k in range(nf)]
+    urgent = [k for k in order if k >= nc]
+    local_k = [k for k in order if k < nc]
+
+    def facet_at(k):
+        row = lax.rem(my_f // nc + k // nc, ny)
+        return row * nc + lax.rem(my_f + k % nc, nc)
+
+    def greet(k, t, b):
         pl.semaphore_signal(
-            barrier, inc=1, device_id={"facet": f, "team": t, "sub": my_b}, device_id_type=MESH
+            barrier, inc=1, device_id={"facet": facet_at(k), "team": t, "sub": b}, device_id_type=MESH
         )
-        return carry
-
-    lax.fori_loop(0, n - 1, greet, 0)
-    for f in range(nf):
-        pl.semaphore_signal(
-            barrier, inc=1, device_id={"facet": f, "team": my_t, "sub": other}, device_id_type=MESH
-        )
-
+
+    for t in range(nt):
+        for k in order:
+            if k:
+                greet(k, t, my_b)
+            else:
+                pl.when(my_t != t)(functools.partial(greet, k, t, my_b))
+        if t == 0:
+            greet(0, my_t, other)
     base_c, base_s = sincos(iota((M, LANES), 0) * iota((M, LANES), 1), length)
     lane_row = iota((1, LANES), 1)
 
     fetches[0].wait()
+    fetches[1].wait()
 
     def column_weights(shift_v):
         pc, ps = sincos(lane_row * shift_v, length)
@@ -120,33 +125,34 @@
         return cat([cat([c, s], 1), cat([-s, c], 1)], 0)
 
     scale = 1.0 / math.sqrt(length)
-    for a in range(nf):
-        shift_v = sub_off[1, a * nb + my_b]
-        wt_near[a] = column_weights(shift_v)
-        c, s = sincos(iota((tiles, M), 0) * (iota((tiles, M), 1) + shift_v), tiles)
-        tw1[a, 0] = c * scale
-        tw1[a, 1] = s * scale
-    fetches[1].wait()
     x = [
         cat([rows[0, c, :, k * LANES : (k + 1) * LANES].astype(F32) for k in range(tiles)], 0)
         for c in range(2)
     ]
     x = cat(x, 1).astype(BF)
-    for a in range(nf):
-        y = mm_nt(x, wt_near[a])
+
+    def spectrum(k):
+        shift_v = sub_off[1, facet_at(k) * nb + my_b]
+        wt_near[k] = column_weights(shift_v)
+        y = mm_nt(x, wt_near[k])
+        c, s = sincos(iota((tiles, M), 0) * (iota((tiles, M), 1) + shift_v), tiles)
+        tw1[k, 0] = c * scale
+        tw1[k, 1] = s * scale
         acc = [None] * 4
-        for k in range(tiles):
-            yr = y[k * rdev : (k + 1) * rdev, :M]
-            yi = y[k * rdev : (k + 1) * rdev, M:]
-            c = tw1[a, 0, k : k + 1, :]
-            s = tw1[a, 1, k : k + 1, :]
-            q = 2 * (k % 2)
+        for j in range(tiles):
+            yr = y[j * rdev : (j + 1) * rdev, :M]
+            yi = y[j * rdev : (j + 1) * rdev, M:]
+            c = tw1[k, 0, j : j + 1, :]
+            s = tw1[k, 1, j : j + 1, :]
+            q = 2 * (j % 2)
             add_re = yr * c + yi * s
             add_im = yi * c - yr * s
             acc[q] = add_re if acc[q] is None else acc[q] + add_re
             acc[q + 1] = add_im if acc[q + 1] is None else acc[q + 1] + add_im
-        spec_out[a] = cat([acc[0] + acc[2], acc[1] + acc[3]], 1).astype(BF)
-
+        spec_out[k] = cat([acc[0] + acc[2], acc[1] + acc[3]], 1).astype(BF)
+
+    for k in urgent:
+        spectrum(k)
     for i in (2, 3, 4, 5, 6):
         fetches[i].wait()
     live = iota((1, slots), 1) < counts[my_f, my_b, my_t]
@@ -164,38 +170,44 @@
     slot_out[...] = packed
     got_x[my_t] = packed
 
-    pl.semaphore_wait(barrier, n - 1 + nf)
-
-    def copy_x(k):
+    pl.semaphore_wait(barrier, n)
+
+    def copy_x(t):
         return pltpu.make_async_remote_copy(
             src_ref=slot_out,
             dst_ref=got_x.at[my_t],
             send_sem=send_x,
             recv_sem=recv_x.at[my_t],
-            device_id={"facet": my_f, "team": lax.rem(my_t + k, nt), "sub": my_b},
+            device_id={"facet": my_f, "team": t, "sub": my_b},
             device_id_type=MESH,
         )
 
-    def copy1(df, dt):
-        f = lax.rem(my_f + df, nf)
-        t = lax.rem(my_t + dt, nt)
+    def copy1(k, t):
         return pltpu.make_async_remote_copy(
-            src_ref=spec_out.at[f],
+            src_ref=spec_out.at[k],
             dst_ref=got1.at[me],
             send_sem=send1,
-            recv_sem=recv1,
-            device_id={"facet": f, "team": t, "sub": my_b},
+            recv_sem=recv1.at[my_t],
+            device_id={"facet": facet_at(k), "team": t, "sub": my_b},
             device_id_type=MESH,
         )
 
-    for dt in range(1, nt + 1):
-        if dt < nt:
-            copy_x(dt).start()
-        for df in range(nf):
-            df = (df + nf // 2) % nf
-            if df or dt < nt:
-                copy1(df, dt % nt).start()
-    got1[me] = spec_out[my_f]
+    def send_specs(ks, t):
+        for k in ks:
+            if k:
+                copy1(k, t).start()
+            else:
+                pl.when(my_t != t)(lambda: copy1(0, t).start())
+
+    def send_slots(t):
+        pl.when(my_t != t)(lambda: copy_x(t).start())
+
+    send_specs(urgent, 0)
+    send_slots(0)
+    for k in local_k:
+        spectrum(k)
+    send_specs(local_k, 0)
+    got1[me] = spec_out[0]
 
     for i in (7, 8, 9, 10):
         fetches[i].wait()
@@ -223,12 +235,15 @@
     ah = cat([at[:, :size], -at[:, size:]], 1).astype(BF)
     ec, es = sincos(iota((n * rdev, M), 1) * row_cc, length)
 
+    for t in range(1, nt):
+        send_specs(order, t)
+        send_slots(t)
     half = tiles // nb
     scale_b = 1.0 / (math.sqrt(M) * size)
     tile_no = iota((half, M), 0) + my_b * half
     for far in range(2):
         for a in range(nf):
-            shift_v = sub_off[1, a * nb + (other if far else my_b)]
+            shift_v = sub_off[1, facet_at(a) * nb + (other if far else my_b)]
             if far:
                 wt_far[a] = column_weights(shift_v)
             m_no = iota((half, M), 1)
@@ -270,8 +285,10 @@
     amap = aterm[...].astype(F32)
     amap = cat([amap, amap], 1)
 
-    done = got1.at[pl.ds(0, n - 1)]
-    pltpu.make_async_copy(done, done, recv1).wait()
+    for k in range(nt):
+        src = lax.rem(my_t + k, nt)
+        done = got1.at[pl.ds(0, nf if k else nf - 1)]
+        pltpu.make_async_copy(done, done, recv1.at[src]).wait()
     sp = got1[...].astype(F32).reshape(n * rdev, 2 * M)
     sr = sp[:, :M]
     si = sp[:, M:]
@@ -313,54 +330,58 @@
 
 
     def copy2(k, far):
-        f = lax.rem(my_f + k, nf)
         return pltpu.make_async_remote_copy(
-            src_ref=fold_out.at[f],
+            src_ref=fold_out.at[facet_at(k)],
             dst_ref=got2.at[far, my_f],
             send_sem=send2,
-            recv_sem=recv2.at[far],
-            device_id={"facet": f, "team": my_t, "sub": other if far else my_b},
+            recv_sem=recv2.at[min(k // nc, 1) + far],
+            device_id={"facet": facet_at(k), "team": my_t, "sub": other if far else my_b},
             device_id_type=MESH,
         )
 
-    for k in range(1, nf + 1):
-        copy2(k % nf, 1).start()
-    for k in range(1, nf):
-        copy2(k, 0).start()
+    for k in urgent:
+        copy2(k, 1).start()
+    for k in local_k:
+        copy2(k, 1).start()
+    for k in urgent + local_k:
+        if k:
+            copy2(k, 0).start()
     got2[0, my_f] = fold_out[my_f]
 
-    def update(far):
-        left = []
-        for a in range(nf):
-            g = got2[far, a].astype(F32)
+    def update(total, far, ks):
+        for k in ks:
+            g = got2[far, facet_at(k)].astype(F32)
             gr = g[:, :M]
             gi = g[:, M:]
             parts = []
-            for k in range(half):
-                c = tw2[far, a, 0, k : k + 1, :]
-                s = tw2[far, a, 1, k : k + 1, :]
+            for j in range(half):
+                c = tw2[far, k, 0, j : j + 1, :]
+                s = tw2[far, k, 1, j : j + 1, :]
                 parts.append(cat([gr * c - gi * s, gr * s + gi * c], 1))
-            left.append(cat(parts, 0).astype(BF))
-        wts = wt_far if far else wt_near
-        total = None
-        for a in range(nf):
-            y = mm(left[a], wts[a])
+            y = mm(cat(parts, 0).astype(BF), (wt_far if far else wt_near)[k])
             total = y if total is None else total + y
         return total
 
-    done = got2.at[0, pl.ds(0, nf - 1)]
-    pltpu.make_async_copy(done, done, recv2.at[0]).wait()
-    near = update(0)
-    done = got2.at[1]
-    pltpu.make_async_copy(done, done, recv2.at[1]).wait()
-    total = near + update(1)
+    def arrived(which, count):
+        done = got1.at[pl.ds(0, count)]
+        pltpu.make_async_copy(done, done, recv2.at[which]).wait()
+
+    if nc > 1:
+        arrived(0, nc - 1)
+    total = update(None, 0, local_k)
+    arrived(1, nf)
+    total = update(total, 1, local_k)
+    total = update(total, 0, urgent)
+    if ny > 1:
+        arrived(2, nf - nc)
+    total = update(total, 1, urgent)
     for k in range(half):
         rng = slice(k * rdev, (k + 1) * rdev)
         lanes = slice(k * LANES, (k + 1) * LANES)
         out[0, 0, :, lanes] = total[rng, :LANES]
         out[0, 1, :, lanes] = total[rng, LANES:]
-    for k in range(1, nt):
-        copy_x(k).wait_send()
+    sent = got1.at[pl.ds(0, nt - 1)]
+    pltpu.make_async_copy(sent, sent, send_x).wait()
     sent = got1.at[pl.ds(0, n - 1)]
     pltpu.make_async_copy(sent, sent, send1).wait()
     sent = got1.at[pl.ds(0, 2 * nf - 1)]
@@ -422,7 +443,7 @@
             vmem((nt, size, slots), F32),
             vmem((nt, size, slots), F32),
             vmem((nt, 8, slots), F32),
-            dma, dma, dma, dma((nt,)), dma, dma((nb,)), dma((11,)),
+            dma, dma((nt,)), dma, dma((nt,)), dma, dma((3,)), dma((11,)),
         ],
         compiler_params=pltpu.CompilerParams(
             collective_id=0, has_side_effects=True

time: 16.4 us -> 16 us (0.976)
  Pallas kernels: 15.5 us -> 15.2 us
    pallas_call x1, Pallas kernels: 15.5 us -> 15.2 us  [local(): pl.pallas_call(functools.partial(body, dims), out_shape=pltpu.VMEM((1, 2,...]
where the time goes in v3:
time: 16 us; the launch traced here: 15.9 us
  Pallas kernels  15.2 us (95%)
  local copies, waits for them, and re-layouts  0.66 us (4%)
    pallas_call x1, Pallas kernels, local(): pl.pallas_call(functools.partial(body, dims), out_shape=pltpu.VMEM((1, 2,...  15.2 us
    unnamed x1, local copies, waits for them, and re-layouts  0.66 us

profile of v3, /device:TPU:0, one launch (start us, length us, event | category | flops | bytes accessed | tf_op | source)
XLA Modules:
  0.0 15.9 jit_solution(10089259306008439751)
XLA Ops:
  0.0 15.2 %shard_map.109 = f32[1,2,8,2048]{3,2,1,0:T(8,128)S(1)} custom-call(s32[2,8]{1,0:T(2,128)} %bitcast.3, s32[2,4]{1,0:T(2,128)} %bitcast.4, s32[4,2,4]{2,1,0:T(2,128)} %refs_2_.1, bf16[1,2,8,4096]{3,2,1,0:T(8,128)(2,1)} %refs_3_.1, bf16[1,2,256,256]{3,2,1,0:T(8,128)(2,1)} %refs_4_.1, s32[1,2,1,2,256]{4,3,2,1,0:T(2,128)} %refs_5_.1, ...), custom_call_target="tpu_custom_call" | custom-call | tf_op jit(solution)/shard_map/pallas_call | solution.py:419
  15.2 0.7 %copy.13 = f32[1,2,8,2048]{3,2,1,0:T(8,128)} copy(f32[1,2,8,2048]{3,2,1,0:T(8,128)S(1)} %shard_map.109) | data formatting | bytes 262144

commit v4 on v3

--- a/solution.py
+++ b/solution.py
@@ -52,14 +52,14 @@
 
 
 def body(dims, *refs):
-    (sub_hbm, fac_hbm, cnt_hbm, rows_hbm, aterm_hbm, cells_hbm, obs_hbm, wt_hbm, kk_hbm, kt_hbm, kb_hbm) = refs[:11]
-    out = refs[11]
+    (sub_hbm, fac_hbm, cnt_hbm, rows_hbm, aterm_hbm, cells_hbm, obs_hbm, wt_hbm, kk_hbm, kt_hbm) = refs[:10]
+    out = refs[10]
     (
-        sub_off, fac_off, counts, rows, aterm, cells, observed, weights, kk, kt, kb,
+        sub_off, fac_off, counts, rows, aterm, cells, observed, weights, kk, kt,
         spec_out, got1, slot_out, got_x, fold_out, got2,
-        tw1, tw2, wt_near, wt_far, fine, col_w, row_c, row_s, res,
+        tw1, tw2, wt_near, wt_far, fine, col_w, row_c, row_s,
         send1, recv1, send_x, recv_x, send2, recv2, in_sem,
-    ) = refs[12:]
+    ) = refs[11:]
     nf, nt, nb, length, size, rdev = dims
     rall = rdev * nt
     n = nf * nt
@@ -83,9 +83,8 @@
         pltpu.make_async_copy(kt_hbm, kt, in_sem.at[7]),
         pltpu.make_async_copy(kk_hbm, kk, in_sem.at[8]),
         pltpu.make_async_copy(aterm_hbm.at[0, my_b], aterm, in_sem.at[9]),
-        pltpu.make_async_copy(kb_hbm, kb, in_sem.at[10]),
     ]
-    for fetch in fetches:
+    for fetch in fetches[:7]:
         fetch.start()
 
     barrier = pltpu.get_barrier_semaphore()
@@ -117,6 +116,8 @@
 
     fetches[0].wait()
     fetches[1].wait()
+    for fetch in fetches[7:]:
+        fetch.start()
 
     def column_weights(shift_v):
         pc, ps = sincos(lane_row * shift_v, length)
@@ -187,7 +188,7 @@
             src_ref=spec_out.at[k],
             dst_ref=got1.at[me],
             send_sem=send1,
-            recv_sem=recv1.at[my_t],
+            recv_sem=recv1,
             device_id={"facet": facet_at(k), "team": t, "sub": my_b},
             device_id_type=MESH,
         )
@@ -202,14 +203,14 @@
     def send_slots(t):
         pl.when(my_t != t)(lambda: copy_x(t).start())
 
+    send_slots(0)
     send_specs(urgent, 0)
-    send_slots(0)
     for k in local_k:
         spectrum(k)
     send_specs(local_k, 0)
     got1[me] = spec_out[0]
 
-    for i in (7, 8, 9, 10):
+    for i in (7, 8, 9):
         fetches[i].wait()
     shift_u = sub_off[0, my_f * nb + my_b]
     step = length // rall
@@ -236,8 +237,8 @@
     ec, es = sincos(iota((n * rdev, M), 1) * row_cc, length)
 
     for t in range(1, nt):
+        send_slots(t)
         send_specs(order, t)
-        send_slots(t)
     half = tiles // nb
     scale_b = 1.0 / (math.sqrt(M) * size)
     tile_no = iota((half, M), 0) + my_b * half
@@ -275,20 +276,14 @@
                     row_c[k, rng, :] = c
                     row_s[k, rng, :] = s
                 else:
-                    cb = c.astype(BF)
-                    sb = s.astype(BF)
-                    low = slice(size + q * FINE, size + (q + 1) * FINE)
-                    col_w[k, rng, :slots] = cb
-                    col_w[k, rng, slots:] = -sb
-                    col_w[k, low, :slots] = sb
-                    col_w[k, low, slots:] = cb
+                    col_w[k, 0, rng, :] = c.astype(BF)
+                    col_w[k, 1, rng, :] = (c - s).astype(BF)
+                    col_w[k, 2, rng, :] = (c + s).astype(BF)
     amap = aterm[...].astype(F32)
     amap = cat([amap, amap], 1)
 
-    for k in range(nt):
-        src = lax.rem(my_t + k, nt)
-        done = got1.at[pl.ds(0, nf if k else nf - 1)]
-        pltpu.make_async_copy(done, done, recv1.at[src]).wait()
+    done = got1.at[pl.ds(0, n - 1)]
+    pltpu.make_async_copy(done, done, recv1).wait()
     sp = got1[...].astype(F32).reshape(n * rdev, 2 * M)
     sr = sp[:, :M]
     si = sp[:, M:]
@@ -297,13 +292,18 @@
     tr = t[:, :size]
     ti = t[:, size:]
     image = mm(a_mat, cat([t, cat([-ti, tr], 1)], 0))
-    weighted = (amap * image).astype(BF)
-    grid = None
+    image = amap * image
+    image_re = image[:, :size]
+    image_im = image[:, size:]
+    w_both = (image_re + image_im).astype(BF)
+    w_re = image_re.astype(BF)
+    w_im = image_im.astype(BF)
+    left = [[], [], []]
     for k in range(nt):
         src = lax.rem(my_t + k, nt)
-        z = mm(weighted, col_w[k])
-        zr = z[:, :slots]
-        zi = z[:, slots:]
+        z_both = mm(w_both, col_w[k, 0])
+        zr = z_both - mm(w_im, col_w[k, 1])
+        zi = z_both - mm(w_re, col_w[k, 2])
         rc = row_c[k]
         rs = row_s[k]
         pred_re = jnp.sum(rc * zr + rs * zi, 0, keepdims=True) * (1.0 / size)
@@ -311,18 +311,17 @@
         info = got_x[src].astype(F32)
         res_re = info[6:7, :] * (info[4:5, :] - pred_re)
         res_im = info[6:7, :] * (info[5:6, :] - pred_im)
-        res[k, 0:1, :] = res_re
-        res[k, 1:2, :] = res_im
-    for k in range(nt):
-        rc = row_c[k]
-        rs = row_s[k]
-        res_re = res[k, 0:1, :]
-        res_im = res[k, 1:2, :]
-        left = cat([rc * res_re - rs * res_im, rc * res_im + rs * res_re], 1).astype(BF)
-        part = mm_nt(left, col_w[k])
-        grid = part if grid is None else grid + part
+        left_re = rc * res_re - rs * res_im
+        left_im = rc * res_im + rs * res_re
+        left[0].append((left_re + left_im).astype(BF))
+        left[1].append(left_re.astype(BF))
+        left[2].append(left_im.astype(BF))
+    prod = [
+        mm_nt(cat(left[c], 1), cat([col_w[k, c] for k in range(nt)], 1)) for c in range(3)
+    ]
+    grid = cat([prod[0] - prod[2], prod[0] - prod[1]], 1)
     v = (amap * grid).astype(BF)
-    u = mm(v, kb[...]).astype(BF)
+    u = mm_nt(v, kk[...]).astype(BF)
     ur = u[:, :M]
     ui = u[:, M:]
     part = mm(ah, cat([u, cat([-ui, ur], 1)], 0))
@@ -394,8 +393,7 @@
     ks = np.sin(angle) / math.sqrt(M)
     kk = np.block([[kc, ks], [-ks, kc]])
     kt = np.concatenate([kc.T, ks.T], 1)
-    kb = np.block([[kc.T, -ks.T], [ks.T, kc.T]])
-    return [np.asarray(v, np.float32).astype(ml_dtypes.bfloat16) for v in (kk, kt, kb)]
+    return [np.asarray(v, np.float32).astype(ml_dtypes.bfloat16) for v in (kk, kt)]
 
 
 def local(facet_rows, sub_offsets, facet_offsets, aterm, cells, observed, weights, counts):
@@ -419,7 +417,7 @@
     return pl.pallas_call(
         functools.partial(body, dims),
         out_shape=pltpu.VMEM((1, 2, rdev, length // nb), F32),
-        in_specs=[hbm] * 11,
+        in_specs=[hbm] * 10,
         out_specs=pl.BlockSpec(memory_space=pltpu.VMEM),
         scratch_shapes=[
             *[pltpu.SMEM(v.shape, v.dtype) for v in operands[:3]],
@@ -439,11 +437,10 @@
             vmem((nf, 2 * M, 2 * LANES), BF),
             vmem((nf, 2 * M, 2 * LANES), BF),
             vmem((2, size // FINE, slots), F32),
-            vmem((nt, 2 * size, 2 * slots), BF),
+            vmem((nt, 3, size, slots), BF),
             vmem((nt, size, slots), F32),
             vmem((nt, size, slots), F32),
-            vmem((nt, 8, slots), F32),
-            dma, dma((nt,)), dma, dma((nt,)), dma, dma((3,)), dma((11,)),
+            dma, dma, dma, dma((nt,)), dma, dma((3,)), dma((10,)),
         ],
         compiler_params=pltpu.CompilerParams(
             collective_id=0, has_side_effects=True

time: 16 us -> 15.9 us (level)
  no operation moved by 1% of the time
where the time goes in v4:
time: 15.9 us; the launch traced here: 15.8 us
  Pallas kernels  15.1 us (95%)
  local copies, waits for them, and re-layouts  0.66 us (4%)
    pallas_call x1, Pallas kernels, local(): pl.pallas_call(functools.partial(body, dims), out_shape=pltpu.VMEM((1, 2,...  15.1 us
    unnamed x1, local copies, waits for them, and re-layouts  0.66 us

profile of v4, /device:TPU:0, one launch (start us, length us, event | category | flops | bytes accessed | tf_op | source)
XLA Modules:
  0.0 15.8 jit_solution(14033209318558213925)
XLA Ops:
  0.0 15.1 %shard_map.100 = f32[1,2,8,2048]{3,2,1,0:T(8,128)S(1)} custom-call(s32[2,8]{1,0:T(2,128)} %bitcast.3, s32[2,4]{1,0:T(2,128)} %bitcast.4, s32[4,2,4]{2,1,0:T(2,128)} %refs_2_.1, bf16[1,2,8,4096]{3,2,1,0:T(8,128)(2,1)} %refs_3_.1, bf16[1,2,256,256]{3,2,1,0:T(8,128)(2,1)} %refs_4_.1, s32[1,2,1,2,256]{4,3,2,1,0:T(2,128)} %refs_5_.1, ...), custom_call_target="tpu_custom_call" | custom-call | tf_op jit(solution)/shard_map/pallas_call | solution.py:417
  15.1 0.7 %copy.12 = f32[1,2,8,2048]{3,2,1,0:T(8,128)} copy(f32[1,2,8,2048]{3,2,1,0:T(8,128)S(1)} %shard_map.100) | data formatting | bytes 262144

commit v5 on v4

--- a/solution.py
+++ b/solution.py
@@ -14,6 +14,7 @@
 LANES = 128
 FINE = 16
 HALF_BITS = 5
+PIECES = 4
 TWO_PI = 2.0 * math.pi
 BF = jnp.bfloat16
 F32 = jnp.float32
@@ -80,11 +81,19 @@
         pltpu.make_async_copy(cells_hbm.at[0, my_b, 0], cells, in_sem.at[4]),
         pltpu.make_async_copy(obs_hbm.at[0, my_b, 0], observed, in_sem.at[5]),
         pltpu.make_async_copy(wt_hbm, weights, in_sem.at[6]),
-        pltpu.make_async_copy(kt_hbm, kt, in_sem.at[7]),
-        pltpu.make_async_copy(kk_hbm, kk, in_sem.at[8]),
-        pltpu.make_async_copy(aterm_hbm.at[0, my_b], aterm, in_sem.at[9]),
+        pltpu.make_async_copy(kt_hbm, kt, in_sem.at[0]),
+        pltpu.make_async_copy(kk_hbm, kk, in_sem.at[1]),
+        pltpu.make_async_copy(aterm_hbm.at[0, my_b], aterm, in_sem.at[7]),
     ]
-    for fetch in fetches[:7]:
+    fetches[0].start()
+    piece = length // PIECES
+    for c in range(2):
+        for q in range(PIECES):
+            lanes = pl.ds(q * piece, piece)
+            pltpu.make_async_copy(
+                rows_hbm.at[0, c, :, lanes], rows.at[0, c, :, lanes], in_sem.at[1]
+            ).start()
+    for fetch in fetches[2:7]:
         fetch.start()
 
     barrier = pltpu.get_barrier_semaphore()
@@ -298,8 +307,7 @@
     w_both = (image_re + image_im).astype(BF)
     w_re = image_re.astype(BF)
     w_im = image_im.astype(BF)
-    left = [[], [], []]
-    for k in range(nt):
+    def degrid(k):
         src = lax.rem(my_t + k, nt)
         z_both = mm(w_both, col_w[k, 0])
         zr = z_both - mm(w_im, col_w[k, 1])
@@ -311,14 +319,23 @@
         info = got_x[src].astype(F32)
         res_re = info[6:7, :] * (info[4:5, :] - pred_re)
         res_im = info[6:7, :] * (info[5:6, :] - pred_im)
+        rc = rc.astype(BF)
+        rs = rs.astype(BF)
+        res_re = jnp.broadcast_to(res_re.astype(BF), (size, slots))
+        res_im = jnp.broadcast_to(res_im.astype(BF), (size, slots))
         left_re = rc * res_re - rs * res_im
         left_im = rc * res_im + rs * res_re
-        left[0].append((left_re + left_im).astype(BF))
-        left[1].append(left_re.astype(BF))
-        left[2].append(left_im.astype(BF))
-    prod = [
-        mm_nt(cat(left[c], 1), cat([col_w[k, c] for k in range(nt)], 1)) for c in range(3)
-    ]
+        return [left_re + left_im, left_re, left_im]
+
+    left = [None] * nt
+    prod = [None] * 3
+    for k in range(nt + 1):
+        if k < nt:
+            left[k] = degrid(k)
+        if k:
+            for c in range(3):
+                part = mm_nt(left[k - 1][c], col_w[k - 1, c])
+                prod[c] = part if prod[c] is None else prod[c] + part
     grid = cat([prod[0] - prod[2], prod[0] - prod[1]], 1)
     v = (amap * grid).astype(BF)
     u = mm_nt(v, kk[...]).astype(BF)
@@ -440,7 +457,7 @@
             vmem((nt, 3, size, slots), BF),
             vmem((nt, size, slots), F32),
             vmem((nt, size, slots), F32),
-            dma, dma, dma, dma((nt,)), dma, dma((3,)), dma((10,)),
+            dma, dma, dma, dma((nt,)), dma, dma((3,)), dma((8,)),
         ],
         compiler_params=pltpu.CompilerParams(
             collective_id=0, has_side_effects=True

time: 15.9 us -> 15.9 us (level)
  no operation moved by 1% of the time
where the time goes in v5:
time: 15.9 us; the launch traced here: 15.8 us
  Pallas kernels  15.1 us (95%)
  local copies, waits for them, and re-layouts  0.66 us (4%)
    pallas_call x1, Pallas kernels, local(): pl.pallas_call(functools.partial(body, dims), out_shape=pltpu.VMEM((1, 2,...  15.1 us
    unnamed x1, local copies, waits for them, and re-layouts  0.66 us

profile of v5, /device:TPU:0, one launch (start us, length us, event | category | flops | bytes accessed | tf_op | source)
XLA Modules:
  0.0 15.8 jit_solution(3572434928248340253)
XLA Ops:
  0.0 15.1 %shard_map.100 = f32[1,2,8,2048]{3,2,1,0:T(8,128)S(1)} custom-call(s32[2,8]{1,0:T(2,128)} %bitcast.3, s32[2,4]{1,0:T(2,128)} %bitcast.4, s32[4,2,4]{2,1,0:T(2,128)} %refs_2_.1, bf16[1,2,8,4096]{3,2,1,0:T(8,128)(2,1)} %refs_3_.1, bf16[1,2,256,256]{3,2,1,0:T(8,128)(2,1)} %refs_4_.1, s32[1,2,1,2,256]{4,3,2,1,0:T(2,128)} %refs_5_.1, ...), custom_call_target="tpu_custom_call" | custom-call | tf_op jit(solution)/shard_map/pallas_call | solution.py:434
  15.1 0.7 %copy.12 = f32[1,2,8,2048]{3,2,1,0:T(8,128)} copy(f32[1,2,8,2048]{3,2,1,0:T(8,128)S(1)} %shard_map.100) | data formatting | bytes 262144

commit v6 on v5

--- a/solution.py
+++ b/solution.py
@@ -59,7 +59,7 @@
         sub_off, fac_off, counts, rows, aterm, cells, observed, weights, kk, kt,
         spec_out, got1, slot_out, got_x, fold_out, got2,
         tw1, tw2, wt_near, wt_far, fine, col_w, row_c, row_s,
-        send1, recv1, send_x, recv_x, send2, recv2, in_sem,
+        send1, recv1, send_x, recv_x, send2, recv2, in_sem, ready,
     ) = refs[11:]
     nf, nt, nb, length, size, rdev = dims
     rall = rdev * nt
@@ -112,14 +112,17 @@
             barrier, inc=1, device_id={"facet": facet_at(k), "team": t, "sub": b}, device_id_type=MESH
         )
 
-    for t in range(nt):
+    def greet_team(t):
         for k in order:
-            if k:
-                greet(k, t, my_b)
-            else:
-                pl.when(my_t != t)(functools.partial(greet, k, t, my_b))
-        if t == 0:
-            greet(0, my_t, other)
+            greet(k, t, my_b)
+
+    for t in reversed(range(1, nt)):
+        pl.when(my_t < t)(functools.partial(greet_team, t))
+    greet(0, my_t, other)
+    for k in order:
+        if k:
+            greet(k, my_t, my_b)
+
     base_c, base_s = sincos(iota((M, LANES), 0) * iota((M, LANES), 1), length)
     lane_row = iota((1, LANES), 1)
 
@@ -180,7 +183,15 @@
     slot_out[...] = packed
     got_x[my_t] = packed
 
-    pl.semaphore_wait(barrier, n)
+    pl.semaphore_wait(barrier, nf * (my_t + 1))
+
+    def report(t):
+        for k in order:
+            pl.semaphore_signal(
+                ready.at[my_t], inc=1,
+                device_id={"facet": facet_at(k), "team": t, "sub": my_b}, device_id_type=MESH,
+            )
+
 
     def copy_x(t):
         return pltpu.make_async_remote_copy(
@@ -214,6 +225,8 @@
 
     send_slots(0)
     send_specs(urgent, 0)
+    for t in range(nt - 1):
+        pl.when(my_t > t)(functools.partial(report, t))
     for k in local_k:
         spectrum(k)
     send_specs(local_k, 0)
@@ -246,6 +259,7 @@
     ec, es = sincos(iota((n * rdev, M), 1) * row_cc, length)
 
     for t in range(1, nt):
+        pl.when(my_t < t)(lambda: pl.semaphore_wait(ready.at[t], nf))
         send_slots(t)
         send_specs(order, t)
     half = tiles // nb
@@ -457,7 +471,7 @@
             vmem((nt, 3, size, slots), BF),
             vmem((nt, size, slots), F32),
             vmem((nt, size, slots), F32),
-            dma, dma, dma, dma((nt,)), dma, dma((3,)), dma((8,)),
+            dma, dma, dma, dma((nt,)), dma, dma((3,)), dma((8,)), pltpu.SemaphoreType.REGULAR((nt,)),
         ],
         compiler_params=pltpu.CompilerParams(
             collective_id=0, has_side_effects=True

time: 15.9 us -> 15.6 us (0.981)
  Pallas kernels: 15.1 us -> 14.8 us
    pallas_call x1, Pallas kernels: 15.1 us -> 14.8 us  [local(): pl.pallas_call(functools.partial(body, dims), out_shape=pltpu.VMEM((1, 2,...]
where the time goes in v6:
time: 15.6 us; the launch traced here: 15.4 us
  Pallas kernels  14.8 us (95%)
  local copies, waits for them, and re-layouts  0.66 us (4%)
    pallas_call x1, Pallas kernels, local(): pl.pallas_call(functools.partial(body, dims), out_shape=pltpu.VMEM((1, 2,...  14.8 us
    unnamed x1, local copies, waits for them, and re-layouts  0.66 us

profile of v6, /device:TPU:0, one launch (start us, length us, event | category | flops | bytes accessed | tf_op | source)
XLA Modules:
  0.0 15.4 jit_solution(8355945023132182864)
XLA Ops:
  0.0 14.8 %shard_map.100 = f32[1,2,8,2048]{3,2,1,0:T(8,128)S(1)} custom-call(s32[2,8]{1,0:T(2,128)} %bitcast.3, s32[2,4]{1,0:T(2,128)} %bitcast.4, s32[4,2,4]{2,1,0:T(2,128)} %refs_2_.1, bf16[1,2,8,4096]{3,2,1,0:T(8,128)(2,1)} %refs_3_.1, bf16[1,2,256,256]{3,2,1,0:T(8,128)(2,1)} %refs_4_.1, s32[1,2,1,2,256]{4,3,2,1,0:T(2,128)} %refs_5_.1, ...), custom_call_target="tpu_custom_call" | custom-call | tf_op jit(solution)/shard_map/pallas_call | solution.py:448
  14.8 0.7 %copy.12 = f32[1,2,8,2048]{3,2,1,0:T(8,128)} copy(f32[1,2,8,2048]{3,2,1,0:T(8,128)S(1)} %shard_map.100) | data formatting | bytes 262144

commit v7 on v6

--- a/solution.py
+++ b/solution.py
@@ -58,7 +58,7 @@
     (
         sub_off, fac_off, counts, rows, aterm, cells, observed, weights, kk, kt,
         spec_out, got1, slot_out, got_x, fold_out, got2,
-        tw1, tw2, wt_near, wt_far, fine, col_w, row_c, row_s,
+        tw1, tw2, wt_near, wt_far, coarse, col_w, row_c, row_s,
         send1, recv1, send_x, recv_x, send2, recv2, in_sem, ready,
     ) = refs[11:]
     nf, nt, nb, length, size, rdev = dims
@@ -234,6 +234,7 @@
 
     for i in (7, 8, 9):
         fetches[i].wait()
+    mirror = size // 2
     shift_u = sub_off[0, my_f * nb + my_b]
     step = length // rall
     scale_g = 1.0 / math.sqrt(rall * nf)
@@ -254,14 +255,20 @@
     a_mat = mm(kt[...], cat([cat([gc, gs], 1), cat([-gs, gc], 1)], 0)).astype(BF)
     p1 = iota((nf * rdev, M), 1)
     hc, hs = sincos(p1 * row_a - (p1 + shift_u) * ((row2 % rdev + my_t * rdev) * step), length)
-    at = mm(cat([hc * scale_g, hs * scale_g], 1).astype(BF), kk[...])
-    ah = cat([at[:, :size], -at[:, size:]], 1).astype(BF)
+    hc = (hc * scale_g).astype(BF)
+    hs = (hs * scale_g).astype(BF)
+    at = mm_nt(cat([cat([hc, -hs], 1), cat([hs, hc], 1)], 0), kt[...])
+    ah = cat([at[: nf * rdev], -at[nf * rdev :]], 1).astype(BF)
     ec, es = sincos(iota((n * rdev, M), 1) * row_cc, length)
 
     for t in range(1, nt):
         pl.when(my_t < t)(lambda: pl.semaphore_wait(ready.at[t], nf))
         send_slots(t)
         send_specs(order, t)
+    flip = (iota((mirror, mirror), 0) + iota((mirror, mirror), 1) == mirror - 1).astype(F32).astype(BF)
+    left_half = mm(aterm[:, :mirror], flip)
+    amap = cat([aterm[:, mirror:].astype(F32), left_half], 1)
+    amap = cat([amap, amap], 1)
     half = tiles // nb
     scale_b = 1.0 / (math.sqrt(M) * size)
     tile_no = iota((half, M), 0) + my_b * half
@@ -276,56 +283,57 @@
             tw2[far, a, 1] = s * scale_b
 
     fine_no = iota((FINE, slots), 0)
-    coarse = size // FINE
-    coarse_no = iota((coarse, slots), 0) * FINE
+    row_no = iota((size // FINE, slots), 0)
+    col_no = iota((mirror // FINE, slots), 0)
     for k in range(nt):
         src = lax.rem(my_t + k, nt)
         if k:
             pltpu.make_async_copy(got_x.at[src], got_x.at[src], recv_x.at[src]).wait()
         pos = got_x[src].astype(F32)[0:4, :].astype(jnp.int32)
         pos = (pos[0:2, :] << HALF_BITS) + pos[2:4, :]
-        for axis in range(2):
-            lo_c, lo_s = sincos(fine_no * pos[axis : axis + 1, :], period)
-            hi_c, hi_s = sincos(coarse_no * pos[axis : axis + 1, :], period)
-            fine[0] = hi_c
-            fine[1] = hi_s
-            for q in range(coarse):
-                c1 = fine[0, q : q + 1, :]
-                s1 = fine[1, q : q + 1, :]
-                c = c1 * lo_c - s1 * lo_s
-                s = s1 * lo_c + c1 * lo_s
-                rng = slice(q * FINE, (q + 1) * FINE)
-                if axis == 0:
-                    row_c[k, rng, :] = c
-                    row_s[k, rng, :] = s
-                else:
-                    col_w[k, 0, rng, :] = c.astype(BF)
-                    col_w[k, 1, rng, :] = (c - s).astype(BF)
-                    col_w[k, 2, rng, :] = (c + s).astype(BF)
-    amap = aterm[...].astype(F32)
-    amap = cat([amap, amap], 1)
+        pos_x = pos[0:1, :]
+        pos_y = pos[1:2, :]
+        lo_c, lo_s = sincos(2 * fine_no * pos_x, 2 * period)
+        hi_c, hi_s = sincos(2 * FINE * row_no * pos_x + (size - 1) * pos_y, 2 * period)
+        coarse[0] = hi_c
+        coarse[1] = hi_s
+        for q in range(size // FINE):
+            c1 = coarse[0, q : q + 1, :]
+            s1 = coarse[1, q : q + 1, :]
+            rng = slice(q * FINE, (q + 1) * FINE)
+            row_c[k, rng, :] = c1 * lo_c - s1 * lo_s
+            row_s[k, rng, :] = s1 * lo_c + c1 * lo_s
+        lo_c, lo_s = sincos((2 * fine_no + 1) * pos_y, 2 * period)
+        hi_c, hi_s = sincos(2 * FINE * col_no * pos_y, 2 * period)
+        coarse[0, : mirror // FINE, :] = hi_c
+        coarse[1, : mirror // FINE, :] = hi_s
+        for q in range(mirror // FINE):
+            c1 = coarse[0, q : q + 1, :]
+            s1 = coarse[1, q : q + 1, :]
+            rng = slice(q * FINE, (q + 1) * FINE)
+            col_w[k, rng, :] = (c1 * lo_c - s1 * lo_s).astype(BF)
+            rng = slice(mirror + q * FINE, mirror + (q + 1) * FINE)
+            col_w[k, rng, :] = (s1 * lo_c + c1 * lo_s).astype(BF)
 
     done = got1.at[pl.ds(0, n - 1)]
     pltpu.make_async_copy(done, done, recv1).wait()
     sp = got1[...].astype(F32).reshape(n * rdev, 2 * M)
     sr = sp[:, :M]
     si = sp[:, M:]
-    turned = cat([sr * ec - si * es, sr * es + si * ec], 1).astype(BF)
-    t = mm(turned, kk[...]).astype(BF)
-    tr = t[:, :size]
-    ti = t[:, size:]
-    image = mm(a_mat, cat([t, cat([-ti, tr], 1)], 0))
+    turn_re = (sr * ec - si * es).astype(BF)
+    turn_im = (sr * es + si * ec).astype(BF)
+    full = mm(a_mat, cat([cat([turn_re, turn_im], 1), cat([-turn_im, turn_re], 1)], 0))
+    image = mm(full.astype(BF), kk[...])
     image = amap * image
-    image_re = image[:, :size]
-    image_im = image[:, size:]
-    w_both = (image_re + image_im).astype(BF)
-    w_re = image_re.astype(BF)
-    w_im = image_im.astype(BF)
+    re_p, re_n, im_p, im_n = (image[:, c * mirror : (c + 1) * mirror] for c in range(4))
+    folded = cat(
+        [cat([re_p + re_n, im_p - im_n], 1), cat([im_p + im_n, re_n - re_p], 1)], 0
+    ).astype(BF)
     def degrid(k):
         src = lax.rem(my_t + k, nt)
-        z_both = mm(w_both, col_w[k, 0])
-        zr = z_both - mm(w_im, col_w[k, 1])
-        zi = z_both - mm(w_re, col_w[k, 2])
+        z = mm(folded, col_w[k])
+        zr = z[:size]
+        zi = z[size:]
         rc = row_c[k]
         rs = row_s[k]
         pred_re = jnp.sum(rc * zr + rs * zi, 0, keepdims=True) * (1.0 / size)
@@ -339,18 +347,19 @@
         res_im = jnp.broadcast_to(res_im.astype(BF), (size, slots))
         left_re = rc * res_re - rs * res_im
         left_im = rc * res_im + rs * res_re
-        return [left_re + left_im, left_re, left_im]
+        return cat([left_re, left_im], 0)
 
     left = [None] * nt
-    prod = [None] * 3
+    prod = None
     for k in range(nt + 1):
         if k < nt:
             left[k] = degrid(k)
         if k:
-            for c in range(3):
-                part = mm_nt(left[k - 1][c], col_w[k - 1, c])
-                prod[c] = part if prod[c] is None else prod[c] + part
-    grid = cat([prod[0] - prod[2], prod[0] - prod[1]], 1)
+            part = mm_nt(left[k - 1], col_w[k - 1])
+            prod = part if prod is None else prod + part
+    cr, sr = prod[:size, :mirror], prod[:size, mirror:]
+    ci, si = prod[size:, :mirror], prod[size:, mirror:]
+    grid = cat([cr - si, cr + si, ci + sr, ci - sr], 1)
     v = (amap * grid).astype(BF)
     u = mm_nt(v, kk[...]).astype(BF)
     ur = u[:, :M]
@@ -422,8 +431,11 @@
     angle = (np.arange(M)[:, None] * np.arange(size)[None, :] % size) * (TWO_PI / size)
     kc = np.cos(angle) / math.sqrt(M)
     ks = np.sin(angle) / math.sqrt(M)
+    kt = np.concatenate([kc.T, ks.T], 1)
+    half = size // 2
+    order = np.concatenate([np.arange(half, size), np.arange(half - 1, -1, -1)])
+    kc, ks = kc[:, order], ks[:, order]
     kk = np.block([[kc, ks], [-ks, kc]])
-    kt = np.concatenate([kc.T, ks.T], 1)
     return [np.asarray(v, np.float32).astype(ml_dtypes.bfloat16) for v in (kk, kt)]
 
 
@@ -468,7 +480,7 @@
             vmem((nf, 2 * M, 2 * LANES), BF),
             vmem((nf, 2 * M, 2 * LANES), BF),
             vmem((2, size // FINE, slots), F32),
-            vmem((nt, 3, size, slots), BF),
+            vmem((nt, size, slots), BF),
             vmem((nt, size, slots), F32),
             vmem((nt, size, slots), F32),
             dma, dma, dma, dma((nt,)), dma, dma((3,)), dma((8,)), pltpu.SemaphoreType.REGULAR((nt,)),

time: 15.6 us -> 15.4 us (0.987)
  Pallas kernels: 14.8 us -> 14.6 us
    pallas_call x1, Pallas kernels: 14.8 us -> 14.6 us  [local(): pl.pallas_call(functools.partial(body, dims), out_shape=pltpu.VMEM((1, 2,...]
where the time goes in v7:
time: 15.4 us; the launch traced here: 15.2 us
  Pallas kernels  14.6 us (95%)
  local copies, waits for them, and re-layouts  0.66 us (4%)
    pallas_call x1, Pallas kernels, local(): pl.pallas_call(functools.partial(body, dims), out_shape=pltpu.VMEM((1, 2,...  14.6 us
    unnamed x1, local copies, waits for them, and re-layouts  0.66 us

profile of v7, /device:TPU:0, one launch (start us, length us, event | category | flops | bytes accessed | tf_op | source)
XLA Modules:
  0.0 15.2 jit_solution(2114739386303189383)
XLA Ops:
  0.0 14.6 %shard_map.100 = f32[1,2,8,2048]{3,2,1,0:T(8,128)S(1)} custom-call(s32[2,8]{1,0:T(2,128)} %bitcast.3, s32[2,4]{1,0:T(2,128)} %bitcast.4, s32[4,2,4]{2,1,0:T(2,128)} %refs_2_.1, bf16[1,2,8,4096]{3,2,1,0:T(8,128)(2,1)} %refs_3_.1, bf16[1,2,256,256]{3,2,1,0:T(8,128)(2,1)} %refs_4_.1, s32[1,2,1,2,256]{4,3,2,1,0:T(2,128)} %refs_5_.1, ...), custom_call_target="tpu_custom_call" | custom-call | tf_op jit(solution)/shard_map/pallas_call | solution.py:460
  14.6 0.7 %copy.12 = f32[1,2,8,2048]{3,2,1,0:T(8,128)} copy(f32[1,2,8,2048]{3,2,1,0:T(8,128)S(1)} %shard_map.100) | data formatting | bytes 262144

commit v8 on v7

--- a/solution.py
+++ b/solution.py
@@ -58,7 +58,7 @@
     (
         sub_off, fac_off, counts, rows, aterm, cells, observed, weights, kk, kt,
         spec_out, got1, slot_out, got_x, fold_out, got2,
-        tw1, tw2, wt_near, wt_far, coarse, col_w, row_c, row_s,
+        tw1, tw2, wt_near, wt_far, coarse, col_w, row_w, row_c, row_s,
         send1, recv1, send_x, recv_x, send2, recv2, in_sem, ready,
     ) = refs[11:]
     nf, nt, nb, length, size, rdev = dims
@@ -77,13 +77,13 @@
         pltpu.make_async_copy(sub_hbm, sub_off, in_sem.at[0]),
         pltpu.make_async_copy(rows_hbm, rows, in_sem.at[1]),
         pltpu.make_async_copy(fac_hbm, fac_off, in_sem.at[2]),
-        pltpu.make_async_copy(cnt_hbm, counts, in_sem.at[3]),
-        pltpu.make_async_copy(cells_hbm.at[0, my_b, 0], cells, in_sem.at[4]),
-        pltpu.make_async_copy(obs_hbm.at[0, my_b, 0], observed, in_sem.at[5]),
-        pltpu.make_async_copy(wt_hbm, weights, in_sem.at[6]),
+        pltpu.make_async_copy(cnt_hbm, counts, in_sem.at[2]),
+        pltpu.make_async_copy(cells_hbm.at[0, my_b, 0], cells, in_sem.at[2]),
+        pltpu.make_async_copy(obs_hbm.at[0, my_b, 0], observed, in_sem.at[2]),
+        pltpu.make_async_copy(wt_hbm, weights, in_sem.at[2]),
         pltpu.make_async_copy(kt_hbm, kt, in_sem.at[0]),
         pltpu.make_async_copy(kk_hbm, kk, in_sem.at[1]),
-        pltpu.make_async_copy(aterm_hbm.at[0, my_b], aterm, in_sem.at[7]),
+        pltpu.make_async_copy(aterm_hbm.at[0, my_b], aterm, in_sem.at[3]),
     ]
     fetches[0].start()
     piece = length // PIECES
@@ -188,7 +188,7 @@
     def report(t):
         for k in order:
             pl.semaphore_signal(
-                ready.at[my_t], inc=1,
+                ready.at[my_t - 1], inc=1,
                 device_id={"facet": facet_at(k), "team": t, "sub": my_b}, device_id_type=MESH,
             )
 
@@ -223,8 +223,8 @@
     def send_slots(t):
         pl.when(my_t != t)(lambda: copy_x(t).start())
 
+    send_specs(urgent, 0)
     send_slots(0)
-    send_specs(urgent, 0)
     for t in range(nt - 1):
         pl.when(my_t > t)(functools.partial(report, t))
     for k in local_k:
@@ -262,7 +262,7 @@
     ec, es = sincos(iota((n * rdev, M), 1) * row_cc, length)
 
     for t in range(1, nt):
-        pl.when(my_t < t)(lambda: pl.semaphore_wait(ready.at[t], nf))
+        pl.when(my_t < t)(lambda: pl.semaphore_wait(ready.at[t - 1], nf))
         send_slots(t)
         send_specs(order, t)
     flip = (iota((mirror, mirror), 0) + iota((mirror, mirror), 1) == mirror - 1).astype(F32).astype(BF)
@@ -301,8 +301,12 @@
             c1 = coarse[0, q : q + 1, :]
             s1 = coarse[1, q : q + 1, :]
             rng = slice(q * FINE, (q + 1) * FINE)
-            row_c[k, rng, :] = c1 * lo_c - s1 * lo_s
-            row_s[k, rng, :] = s1 * lo_c + c1 * lo_s
+            c = c1 * lo_c - s1 * lo_s
+            s = s1 * lo_c + c1 * lo_s
+            row_c[k, rng, :] = c
+            row_s[k, rng, :] = s
+            row_w[k, 0, rng, :] = c.astype(BF)
+            row_w[k, 1, rng, :] = s.astype(BF)
         lo_c, lo_s = sincos((2 * fine_no + 1) * pos_y, 2 * period)
         hi_c, hi_s = sincos(2 * FINE * col_no * pos_y, 2 * period)
         coarse[0, : mirror // FINE, :] = hi_c
@@ -341,8 +345,8 @@
         info = got_x[src].astype(F32)
         res_re = info[6:7, :] * (info[4:5, :] - pred_re)
         res_im = info[6:7, :] * (info[5:6, :] - pred_im)
-        rc = rc.astype(BF)
-        rs = rs.astype(BF)
+        rc = row_w[k, 0]
+        rs = row_w[k, 1]
         res_re = jnp.broadcast_to(res_re.astype(BF), (size, slots))
         res_im = jnp.broadcast_to(res_im.astype(BF), (size, slots))
         left_re = rc * res_re - rs * res_im
@@ -481,9 +485,10 @@
             vmem((nf, 2 * M, 2 * LANES), BF),
             vmem((2, size // FINE, slots), F32),
             vmem((nt, size, slots), BF),
+            vmem((nt, 2, size, slots), BF),
             vmem((nt, size, slots), F32),
             vmem((nt, size, slots), F32),
-            dma, dma, dma, dma((nt,)), dma, dma((3,)), dma((8,)), pltpu.SemaphoreType.REGULAR((nt,)),
+            dma, dma, dma, dma((nt,)), dma, dma((3,)), dma((4,)), pltpu.SemaphoreType.REGULAR((max(nt - 1, 1),)),
         ],
         compiler_params=pltpu.CompilerParams(
             collective_id=0, has_side_effects=True

time: 15.4 us -> 15.3 us (level)
  no operation moved by 1% of the time
where the time goes in v8:
time: 15.3 us; the launch traced here: 15.2 us
  Pallas kernels  14.5 us (95%)
  local copies, waits for them, and re-layouts  0.66 us (4%)
    pallas_call x1, Pallas kernels, local(): pl.pallas_call(functools.partial(body, dims), out_shape=pltpu.VMEM((1, 2,...  14.5 us
    unnamed x1, local copies, waits for them, and re-layouts  0.66 us

profile of v8, /device:TPU:0, one launch (start us, length us, event | category | flops | bytes accessed | tf_op | source)
XLA Modules:
  0.0 15.2 jit_solution(13069625779205414874)
XLA Ops:
  0.0 14.5 %shard_map.100 = f32[1,2,8,2048]{3,2,1,0:T(8,128)S(1)} custom-call(s32[2,8]{1,0:T(2,128)} %bitcast.3, s32[2,4]{1,0:T(2,128)} %bitcast.4, s32[4,2,4]{2,1,0:T(2,128)} %refs_2_.1, bf16[1,2,8,4096]{3,2,1,0:T(8,128)(2,1)} %refs_3_.1, bf16[1,2,256,256]{3,2,1,0:T(8,128)(2,1)} %refs_4_.1, s32[1,2,1,2,256]{4,3,2,1,0:T(2,128)} %refs_5_.1, ...), custom_call_target="tpu_custom_call" | custom-call | tf_op jit(solution)/shard_map/pallas_call | solution.py:464
  14.5 0.7 %copy.12 = f32[1,2,8,2048]{3,2,1,0:T(8,128)} copy(f32[1,2,8,2048]{3,2,1,0:T(8,128)S(1)} %shard_map.100) | data formatting | bytes 262144

commit v9 on v8

--- a/solution.py
+++ b/solution.py
@@ -14,7 +14,7 @@
 LANES = 128
 FINE = 16
 HALF_BITS = 5
-PIECES = 4
+PIECES = 2
 TWO_PI = 2.0 * math.pi
 BF = jnp.bfloat16
 F32 = jnp.float32
@@ -59,7 +59,7 @@
         sub_off, fac_off, counts, rows, aterm, cells, observed, weights, kk, kt,
         spec_out, got1, slot_out, got_x, fold_out, got2,
         tw1, tw2, wt_near, wt_far, coarse, col_w, row_w, row_c, row_s,
-        send1, recv1, send_x, recv_x, send2, recv2, in_sem, ready,
+        sent, recv1, recv_x, recv2, in_sem, ready,
     ) = refs[11:]
     nf, nt, nb, length, size, rdev = dims
     rall = rdev * nt
@@ -99,37 +99,44 @@
     barrier = pltpu.get_barrier_semaphore()
     nc = 2 - nf % 2
     ny = nf // nc
-    order = [(k // nc + ny // 2) % ny * nc + k % nc for k in range(nf)]
+    rows_far = [(y + ny // 2) % ny for y in range(ny)]
+    order = [y * nc + c for c in range(nc) for y in rows_far]
+    first = order[:ny]
+    second = order[ny:]
+    local_k = list(range(nc))
     urgent = [k for k in order if k >= nc]
-    local_k = [k for k in order if k < nc]
+    my_c = lax.rem(my_f, nc)
 
     def facet_at(k):
-        row = lax.rem(my_f // nc + k // nc, ny)
-        return row * nc + lax.rem(my_f + k % nc, nc)
+        return lax.rem(my_f // nc + k // nc, ny) * nc + k % nc
 
     def greet(k, t, b):
         pl.semaphore_signal(
             barrier, inc=1, device_id={"facet": facet_at(k), "team": t, "sub": b}, device_id_type=MESH
         )
 
+    def unless_self(k, act):
+        if k < nc:
+            pl.when(my_c != k)(act)
+        else:
+            act()
+
     def greet_team(t):
         for k in order:
             greet(k, t, my_b)
 
     for t in reversed(range(1, nt)):
         pl.when(my_t < t)(functools.partial(greet_team, t))
-    greet(0, my_t, other)
+    pl.semaphore_signal(
+        barrier, inc=1, device_id={"facet": my_f, "team": my_t, "sub": other}, device_id_type=MESH
+    )
     for k in order:
-        if k:
-            greet(k, my_t, my_b)
+        unless_self(k, functools.partial(greet, k, my_t, my_b))
 
     base_c, base_s = sincos(iota((M, LANES), 0) * iota((M, LANES), 1), length)
     lane_row = iota((1, LANES), 1)
 
     fetches[0].wait()
-    fetches[1].wait()
-    for fetch in fetches[7:]:
-        fetch.start()
 
     def column_weights(shift_v):
         pc, ps = sincos(lane_row * shift_v, length)
@@ -138,6 +145,19 @@
         return cat([cat([c, s], 1), cat([-s, c], 1)], 0)
 
     scale = 1.0 / math.sqrt(length)
+
+    def prepare(k):
+        shift_v = sub_off[1, facet_at(k) * nb + my_b]
+        wt_near[k] = column_weights(shift_v)
+        c, s = sincos(iota((tiles, M), 0) * (iota((tiles, M), 1) + shift_v), tiles)
+        tw1[k, 0] = c * scale
+        tw1[k, 1] = s * scale
+
+    for k in first:
+        prepare(k)
+    fetches[1].wait()
+    for fetch in fetches[7:]:
+        fetch.start()
     x = [
         cat([rows[0, c, :, k * LANES : (k + 1) * LANES].astype(F32) for k in range(tiles)], 0)
         for c in range(2)
@@ -145,12 +165,7 @@
     x = cat(x, 1).astype(BF)
 
     def spectrum(k):
-        shift_v = sub_off[1, facet_at(k) * nb + my_b]
-        wt_near[k] = column_weights(shift_v)
         y = mm_nt(x, wt_near[k])
-        c, s = sincos(iota((tiles, M), 0) * (iota((tiles, M), 1) + shift_v), tiles)
-        tw1[k, 0] = c * scale
-        tw1[k, 1] = s * scale
         acc = [None] * 4
         for j in range(tiles):
             yr = y[j * rdev : (j + 1) * rdev, :M]
@@ -164,7 +179,7 @@
             acc[q + 1] = add_im if acc[q + 1] is None else acc[q + 1] + add_im
         spec_out[k] = cat([acc[0] + acc[2], acc[1] + acc[3]], 1).astype(BF)
 
-    for k in urgent:
+    for k in first:
         spectrum(k)
     for i in (2, 3, 4, 5, 6):
         fetches[i].wait()
@@ -197,7 +212,7 @@
         return pltpu.make_async_remote_copy(
             src_ref=slot_out,
             dst_ref=got_x.at[my_t],
-            send_sem=send_x,
+            send_sem=sent,
             recv_sem=recv_x.at[my_t],
             device_id={"facet": my_f, "team": t, "sub": my_b},
             device_id_type=MESH,
@@ -207,7 +222,7 @@
         return pltpu.make_async_remote_copy(
             src_ref=spec_out.at[k],
             dst_ref=got1.at[me],
-            send_sem=send1,
+            send_sem=sent,
             recv_sem=recv1,
             device_id={"facet": facet_at(k), "team": t, "sub": my_b},
             device_id_type=MESH,
@@ -215,22 +230,24 @@
 
     def send_specs(ks, t):
         for k in ks:
-            if k:
+            if k >= nc:
                 copy1(k, t).start()
             else:
-                pl.when(my_t != t)(lambda: copy1(0, t).start())
+                there = jnp.logical_or(my_t != t, my_c != k)
+                pl.when(there)(lambda: copy1(k, t).start())
 
     def send_slots(t):
         pl.when(my_t != t)(lambda: copy_x(t).start())
 
-    send_specs(urgent, 0)
+    send_specs(first, 0)
     send_slots(0)
     for t in range(nt - 1):
         pl.when(my_t > t)(functools.partial(report, t))
-    for k in local_k:
+    for k in second:
+        prepare(k)
         spectrum(k)
-    send_specs(local_k, 0)
-    got1[me] = spec_out[0]
+    send_specs(second, 0)
+    got1[me] = spec_out[my_c]
 
     for i in (7, 8, 9):
         fetches[i].wait()
@@ -376,19 +393,16 @@
         return pltpu.make_async_remote_copy(
             src_ref=fold_out.at[facet_at(k)],
             dst_ref=got2.at[far, my_f],
-            send_sem=send2,
+            send_sem=sent,
             recv_sem=recv2.at[min(k // nc, 1) + far],
             device_id={"facet": facet_at(k), "team": my_t, "sub": other if far else my_b},
             device_id_type=MESH,
         )
 
-    for k in urgent:
+    for k in order:
         copy2(k, 1).start()
-    for k in local_k:
-        copy2(k, 1).start()
-    for k in urgent + local_k:
-        if k:
-            copy2(k, 0).start()
+    for k in order:
+        unless_self(k, lambda: copy2(k, 0).start())
     got2[0, my_f] = fold_out[my_f]
 
     def update(total, far, ks):
@@ -423,12 +437,9 @@
         lanes = slice(k * LANES, (k + 1) * LANES)
         out[0, 0, :, lanes] = total[rng, :LANES]
         out[0, 1, :, lanes] = total[rng, LANES:]
-    sent = got1.at[pl.ds(0, nt - 1)]
-    pltpu.make_async_copy(sent, sent, send_x).wait()
-    sent = got1.at[pl.ds(0, n - 1)]
-    pltpu.make_async_copy(sent, sent, send1).wait()
-    sent = got1.at[pl.ds(0, 2 * nf - 1)]
-    pltpu.make_async_copy(sent, sent, send2).wait()
+    for count in (n - 1, nt - 1, 2 * nf - 1):
+        gone = got1.at[pl.ds(0, count)]
+        pltpu.make_async_copy(gone, gone, sent).wait()
 
 
 def tables(size):
@@ -488,7 +499,7 @@
             vmem((nt, 2, size, slots), BF),
             vmem((nt, size, slots), F32),
             vmem((nt, size, slots), F32),
-            dma, dma, dma, dma((nt,)), dma, dma((3,)), dma((4,)), pltpu.SemaphoreType.REGULAR((max(nt - 1, 1),)),
+            dma, dma, dma((nt,)), dma((3,)), dma((4,)), pltpu.SemaphoreType.REGULAR((max(nt - 1, 1),)),
         ],
         compiler_params=pltpu.CompilerParams(
             collective_id=0, has_side_effects=True

time: 15.3 us -> 15.2 us (level)
  no operation moved by 1% of the time
where the time goes in v9:
time: 15.2 us; the launch traced here: 15 us
  Pallas kernels  14.4 us (95%)
  local copies, waits for them, and re-layouts  0.66 us (4%)
    pallas_call x1, Pallas kernels, local(): pl.pallas_call(functools.partial(body, dims), out_shape=pltpu.VMEM((1, 2,...  14.4 us
    unnamed x1, local copies, waits for them, and re-layouts  0.66 us

profile of v9, /device:TPU:0, one launch (start us, length us, event | category | flops | bytes accessed | tf_op | source)
XLA Modules:
  0.0 15.0 jit_solution(18196844097379866319)
XLA Ops:
  0.0 14.4 %shard_map.100 = f32[1,2,8,2048]{3,2,1,0:T(8,128)S(1)} custom-call(s32[2,8]{1,0:T(2,128)} %bitcast.3, s32[2,4]{1,0:T(2,128)} %bitcast.4, s32[4,2,4]{2,1,0:T(2,128)} %refs_2_.1, bf16[1,2,8,4096]{3,2,1,0:T(8,128)(2,1)} %refs_3_.1, bf16[1,2,256,256]{3,2,1,0:T(8,128)(2,1)} %refs_4_.1, s32[1,2,1,2,256]{4,3,2,1,0:T(2,128)} %refs_5_.1, ...), custom_call_target="tpu_custom_call" | custom-call | tf_op jit(solution)/shard_map/pallas_call | solution.py:475
  14.4 0.7 %copy.12 = f32[1,2,8,2048]{3,2,1,0:T(8,128)} copy(f32[1,2,8,2048]{3,2,1,0:T(8,128)S(1)} %shard_map.100) | data formatting | bytes 262144

commit v10 on v9

--- a/solution.py
+++ b/solution.py
@@ -76,7 +76,7 @@
     fetches = [
         pltpu.make_async_copy(sub_hbm, sub_off, in_sem.at[0]),
         pltpu.make_async_copy(rows_hbm, rows, in_sem.at[1]),
-        pltpu.make_async_copy(fac_hbm, fac_off, in_sem.at[2]),
+        pltpu.make_async_copy(fac_hbm, fac_off, in_sem.at[4]),
         pltpu.make_async_copy(cnt_hbm, counts, in_sem.at[2]),
         pltpu.make_async_copy(cells_hbm.at[0, my_b, 0], cells, in_sem.at[2]),
         pltpu.make_async_copy(obs_hbm.at[0, my_b, 0], observed, in_sem.at[2]),
@@ -86,6 +86,7 @@
         pltpu.make_async_copy(aterm_hbm.at[0, my_b], aterm, in_sem.at[3]),
     ]
     fetches[0].start()
+    fetches[2].start()
     piece = length // PIECES
     for c in range(2):
         for q in range(PIECES):
@@ -93,7 +94,7 @@
             pltpu.make_async_copy(
                 rows_hbm.at[0, c, :, lanes], rows.at[0, c, :, lanes], in_sem.at[1]
             ).start()
-    for fetch in fetches[2:7]:
+    for fetch in fetches[3:7]:
         fetch.start()
 
     barrier = pltpu.get_barrier_semaphore()
@@ -137,6 +138,7 @@
     lane_row = iota((1, LANES), 1)
 
     fetches[0].wait()
+    fetches[2].wait()
 
     def column_weights(shift_v):
         pc, ps = sincos(lane_row * shift_v, length)
@@ -149,7 +151,9 @@
     def prepare(k):
         shift_v = sub_off[1, facet_at(k) * nb + my_b]
         wt_near[k] = column_weights(shift_v)
-        c, s = sincos(iota((tiles, M), 0) * (iota((tiles, M), 1) + shift_v), tiles)
+        m_no = iota((tiles, M), 1)
+        turns = iota((tiles, M), 0) * LANES * (m_no + shift_v) - m_no * fac_off[1, my_f]
+        c, s = sincos(turns, length)
         tw1[k, 0] = c * scale
         tw1[k, 1] = s * scale
 
@@ -181,7 +185,7 @@
 
     for k in first:
         spectrum(k)
-    for i in (2, 3, 4, 5, 6):
+    for i in (3, 4, 5, 6):
         fetches[i].wait()
     live = iota((1, slots), 1) < counts[my_f, my_b, my_t]
     all_wt = weights[0, 0].astype(F32)
@@ -257,13 +261,10 @@
     scale_g = 1.0 / math.sqrt(rall * nf)
     lane = iota((1, n * rdev), 1)
     col_a = jnp.zeros((1, n * rdev), jnp.int32)
-    row = iota((n * rdev, 1), 0)
-    row_cc = jnp.zeros((n * rdev, 1), jnp.int32)
     row2 = iota((nf * rdev, 1), 0)
     row_a = jnp.zeros((nf * rdev, 1), jnp.int32)
     for f in range(nf):
         col_a = jnp.where(lane // rall == f, fac_off[0, f], col_a)
-        row_cc = jnp.where(row // rall == f, fac_off[1, f], row_cc)
         row_a = jnp.where(row2 // rdev == f, fac_off[0, f], row_a)
     p0 = iota((M, n * rdev), 0)
     gc, gs = sincos(p0 * col_a - (p0 + shift_u) * (lane % rall * step), length)
@@ -276,7 +277,6 @@
     hs = (hs * scale_g).astype(BF)
     at = mm_nt(cat([cat([hc, -hs], 1), cat([hs, hc], 1)], 0), kt[...])
     ah = cat([at[: nf * rdev], -at[nf * rdev :]], 1).astype(BF)
-    ec, es = sincos(iota((n * rdev, M), 1) * row_cc, length)
 
     for t in range(1, nt):
         pl.when(my_t < t)(lambda: pl.semaphore_wait(ready.at[t - 1], nf))
@@ -338,12 +338,9 @@
 
     done = got1.at[pl.ds(0, n - 1)]
     pltpu.make_async_copy(done, done, recv1).wait()
-    sp = got1[...].astype(F32).reshape(n * rdev, 2 * M)
-    sr = sp[:, :M]
-    si = sp[:, M:]
-    turn_re = (sr * ec - si * es).astype(BF)
-    turn_im = (sr * es + si * ec).astype(BF)
-    full = mm(a_mat, cat([cat([turn_re, turn_im], 1), cat([-turn_im, turn_re], 1)], 0))
+    got = got1[...].astype(F32).reshape(n * rdev, 2 * M)
+    got = cat([got, cat([-got[:, M:], got[:, :M]], 1)], 0).astype(BF)
+    full = mm(a_mat, got)
     image = mm(full.astype(BF), kk[...])
     image = amap * image
     re_p, re_n, im_p, im_n = (image[:, c * mirror : (c + 1) * mirror] for c in range(4))
@@ -499,7 +496,7 @@
             vmem((nt, 2, size, slots), BF),
             vmem((nt, size, slots), F32),
             vmem((nt, size, slots), F32),
-            dma, dma, dma((nt,)), dma((3,)), dma((4,)), pltpu.SemaphoreType.REGULAR((max(nt - 1, 1),)),
+            dma, dma, dma((nt,)), dma((3,)), dma((5,)), pltpu.SemaphoreType.REGULAR((max(nt - 1, 1),)),
         ],
         compiler_params=pltpu.CompilerParams(
             collective_id=0, has_side_effects=True

time: 15.2 us -> 15.2 us (level)
  no operation moved by 1% of the time
where the time goes in v10:
time: 15.2 us; the launch traced here: 15 us
  Pallas kernels  14.3 us (94%)
  local copies, waits for them, and re-layouts  0.66 us (4%)
    pallas_call x1, Pallas kernels, local(): pl.pallas_call(functools.partial(body, dims), out_shape=pltpu.VMEM((1, 2,...  14.3 us
    unnamed x1, local copies, waits for them, and re-layouts  0.66 us

profile of v10, /device:TPU:0, one launch (start us, length us, event | category | flops | bytes accessed | tf_op | source)
XLA Modules:
  0.0 15.0 jit_solution(3068274323182759465)
XLA Ops:
  0.0 14.3 %shard_map.100 = f32[1,2,8,2048]{3,2,1,0:T(8,128)S(1)} custom-call(s32[2,8]{1,0:T(2,128)} %bitcast.3, s32[2,4]{1,0:T(2,128)} %bitcast.4, s32[4,2,4]{2,1,0:T(2,128)} %refs_2_.1, bf16[1,2,8,4096]{3,2,1,0:T(8,128)(2,1)} %refs_3_.1, bf16[1,2,256,256]{3,2,1,0:T(8,128)(2,1)} %refs_4_.1, s32[1,2,1,2,256]{4,3,2,1,0:T(2,128)} %refs_5_.1, ...), custom_call_target="tpu_custom_call" | custom-call | tf_op jit(solution)/shard_map/pallas_call | solution.py:472
  14.3 0.7 %copy.12 = f32[1,2,8,2048]{3,2,1,0:T(8,128)} copy(f32[1,2,8,2048]{3,2,1,0:T(8,128)S(1)} %shard_map.100) | data formatting | bytes 262144

commit v11 on v10

--- a/solution.py
+++ b/solution.py
@@ -58,7 +58,7 @@
     (
         sub_off, fac_off, counts, rows, aterm, cells, observed, weights, kk, kt,
         spec_out, got1, slot_out, got_x, fold_out, got2,
-        tw1, tw2, wt_near, wt_far, coarse, col_w, row_w, row_c, row_s,
+        tw1, tw2, wt_near, wt_far, coarse, middle, col_w, row_w, row_c, row_s,
         sent, recv1, recv_x, recv2, in_sem, ready,
     ) = refs[11:]
     nf, nt, nb, length, size, rdev = dims
@@ -283,8 +283,9 @@
         send_slots(t)
         send_specs(order, t)
     flip = (iota((mirror, mirror), 0) + iota((mirror, mirror), 1) == mirror - 1).astype(F32).astype(BF)
-    left_half = mm(aterm[:, :mirror], flip)
-    amap = cat([aterm[:, mirror:].astype(F32), left_half], 1)
+    low = mm(flip, aterm[:mirror, :])
+    both = cat([aterm[mirror:, :].astype(F32), low], 0)
+    amap = cat([both[:, mirror:], mm(both[:, :mirror].astype(BF), flip)], 1)
     amap = cat([amap, amap], 1)
     half = tiles // nb
     scale_b = 1.0 / (math.sqrt(M) * size)
@@ -300,7 +301,6 @@
             tw2[far, a, 1] = s * scale_b
 
     fine_no = iota((FINE, slots), 0)
-    row_no = iota((size // FINE, slots), 0)
     col_no = iota((mirror // FINE, slots), 0)
     for k in range(nt):
         src = lax.rem(my_t + k, nt)
@@ -310,32 +310,29 @@
         pos = (pos[0:2, :] << HALF_BITS) + pos[2:4, :]
         pos_x = pos[0:1, :]
         pos_y = pos[1:2, :]
-        lo_c, lo_s = sincos(2 * fine_no * pos_x, 2 * period)
-        hi_c, hi_s = sincos(2 * FINE * row_no * pos_x + (size - 1) * pos_y, 2 * period)
-        coarse[0] = hi_c
-        coarse[1] = hi_s
-        for q in range(size // FINE):
-            c1 = coarse[0, q : q + 1, :]
-            s1 = coarse[1, q : q + 1, :]
-            rng = slice(q * FINE, (q + 1) * FINE)
-            c = c1 * lo_c - s1 * lo_s
-            s = s1 * lo_c + c1 * lo_s
-            row_c[k, rng, :] = c
-            row_s[k, rng, :] = s
-            row_w[k, 0, rng, :] = c.astype(BF)
-            row_w[k, 1, rng, :] = s.astype(BF)
-        lo_c, lo_s = sincos((2 * fine_no + 1) * pos_y, 2 * period)
-        hi_c, hi_s = sincos(2 * FINE * col_no * pos_y, 2 * period)
-        coarse[0, : mirror // FINE, :] = hi_c
-        coarse[1, : mirror // FINE, :] = hi_s
-        for q in range(mirror // FINE):
-            c1 = coarse[0, q : q + 1, :]
-            s1 = coarse[1, q : q + 1, :]
-            rng = slice(q * FINE, (q + 1) * FINE)
-            col_w[k, rng, :] = (c1 * lo_c - s1 * lo_s).astype(BF)
-            rng = slice(mirror + q * FINE, mirror + (q + 1) * FINE)
-            col_w[k, rng, :] = (s1 * lo_c + c1 * lo_s).astype(BF)
-
+        mid_c, mid_s = sincos((size - 1) * (pos_x + pos_y), 2 * period)
+        middle[k, 0:1, :] = mid_c
+        middle[k, 1:2, :] = mid_s
+        for axis, place in enumerate((pos_x, pos_y)):
+            lo_c, lo_s = sincos((2 * fine_no + 1) * place, 2 * period)
+            hi_c, hi_s = sincos(2 * FINE * col_no * place, 2 * period)
+            coarse[0] = hi_c
+            coarse[1] = hi_s
+            for q in range(mirror // FINE):
+                c1 = coarse[0, q : q + 1, :]
+                s1 = coarse[1, q : q + 1, :]
+                c = c1 * lo_c - s1 * lo_s
+                s = s1 * lo_c + c1 * lo_s
+                rng = slice(q * FINE, (q + 1) * FINE)
+                low = slice(mirror + q * FINE, mirror + (q + 1) * FINE)
+                if axis == 0:
+                    row_c[k, rng, :] = c
+                    row_s[k, rng, :] = s
+                    row_w[k, rng, :] = c.astype(BF)
+                    row_w[k, low, :] = s.astype(BF)
+                else:
+                    col_w[k, rng, :] = c.astype(BF)
+                    col_w[k, low, :] = s.astype(BF)
     done = got1.at[pl.ds(0, n - 1)]
     pltpu.make_async_copy(done, done, recv1).wait()
     got = got1[...].astype(F32).reshape(n * rdev, 2 * M)
@@ -346,26 +343,30 @@
     re_p, re_n, im_p, im_n = (image[:, c * mirror : (c + 1) * mirror] for c in range(4))
     folded = cat(
         [cat([re_p + re_n, im_p - im_n], 1), cat([im_p + im_n, re_n - re_p], 1)], 0
-    ).astype(BF)
+    )
+    a, b, c, d = (folded[q * mirror : (q + 1) * mirror] for q in range(4))
+    folded = cat([a + b, a - b, c + d, c - d], 0).astype(BF)
     def degrid(k):
         src = lax.rem(my_t + k, nt)
         z = mm(folded, col_w[k])
-        zr = z[:size]
-        zi = z[size:]
+        re_e, re_o, im_e, im_o = (z[q * mirror : (q + 1) * mirror] for q in range(4))
         rc = row_c[k]
         rs = row_s[k]
-        pred_re = jnp.sum(rc * zr + rs * zi, 0, keepdims=True) * (1.0 / size)
-        pred_im = jnp.sum(rc * zi - rs * zr, 0, keepdims=True) * (1.0 / size)
+        mid_c = middle[k, 0:1, :]
+        mid_s = middle[k, 1:2, :]
+        sum_re = jnp.sum(rc * re_e + rs * im_o, 0, keepdims=True) * (1.0 / size)
+        sum_im = jnp.sum(rc * im_e - rs * re_o, 0, keepdims=True) * (1.0 / size)
+        pred_re = sum_re * mid_c + sum_im * mid_s
+        pred_im = sum_im * mid_c - sum_re * mid_s
         info = got_x[src].astype(F32)
         res_re = info[6:7, :] * (info[4:5, :] - pred_re)
         res_im = info[6:7, :] * (info[5:6, :] - pred_im)
-        rc = row_w[k, 0]
-        rs = row_w[k, 1]
-        res_re = jnp.broadcast_to(res_re.astype(BF), (size, slots))
-        res_im = jnp.broadcast_to(res_im.astype(BF), (size, slots))
-        left_re = rc * res_re - rs * res_im
-        left_im = rc * res_im + rs * res_re
-        return cat([left_re, left_im], 0)
+        turn_re = res_re * mid_c - res_im * mid_s
+        turn_im = res_re * mid_s + res_im * mid_c
+        turn_re = jnp.broadcast_to(turn_re.astype(BF), (size, slots))
+        turn_im = jnp.broadcast_to(turn_im.astype(BF), (size, slots))
+        rows_w = row_w[k]
+        return cat([rows_w * turn_re, rows_w * turn_im], 0)
 
     left = [None] * nt
     prod = None
@@ -375,8 +376,11 @@
         if k:
             part = mm_nt(left[k - 1], col_w[k - 1])
             prod = part if prod is None else prod + part
-    cr, sr = prod[:size, :mirror], prod[:size, mirror:]
-    ci, si = prod[size:, :mirror], prod[size:, mirror:]
+    a, c, b, d = (prod[q * mirror : (q + 1) * mirror] for q in range(4))
+    real = cat([a - d, a + d], 0)
+    imag = cat([b + c, b - c], 0)
+    cr, sr = real[:, :mirror], real[:, mirror:]
+    ci, si = imag[:, :mirror], imag[:, mirror:]
     grid = cat([cr - si, cr + si, ci + sr, ci - sr], 1)
     v = (amap * grid).astype(BF)
     u = mm_nt(v, kk[...]).astype(BF)
@@ -443,10 +447,10 @@
     angle = (np.arange(M)[:, None] * np.arange(size)[None, :] % size) * (TWO_PI / size)
     kc = np.cos(angle) / math.sqrt(M)
     ks = np.sin(angle) / math.sqrt(M)
-    kt = np.concatenate([kc.T, ks.T], 1)
     half = size // 2
     order = np.concatenate([np.arange(half, size), np.arange(half - 1, -1, -1)])
     kc, ks = kc[:, order], ks[:, order]
+    kt = np.concatenate([kc.T, ks.T], 1)
     kk = np.block([[kc, ks], [-ks, kc]])
     return [np.asarray(v, np.float32).astype(ml_dtypes.bfloat16) for v in (kk, kt)]
 
@@ -491,11 +495,12 @@
             vmem((nb, nf, 2, tiles // nb, M), F32),
             vmem((nf, 2 * M, 2 * LANES), BF),
             vmem((nf, 2 * M, 2 * LANES), BF),
-            vmem((2, size // FINE, slots), F32),
+            vmem((2, size // 2 // FINE, slots), F32),
+            vmem((nt, 8, slots), F32),
             vmem((nt, size, slots), BF),
-            vmem((nt, 2, size, slots), BF),
-            vmem((nt, size, slots), F32),
-            vmem((nt, size, slots), F32),
+            vmem((nt, size, slots), BF),
+            vmem((nt, size // 2, slots), F32),
+            vmem((nt, size // 2, slots), F32),
             dma, dma, dma((nt,)), dma((3,)), dma((5,)), pltpu.SemaphoreType.REGULAR((max(nt - 1, 1),)),
         ],
         compiler_params=pltpu.CompilerParams(

time: 15.2 us -> 15.2 us (level)
  no operation moved by 1% of the time
where the time goes in v11:
time: 15.2 us; the launch traced here: 15 us
  Pallas kernels  14.3 us (94%)
  local copies, waits for them, and re-layouts  0.66 us (4%)
    pallas_call x1, Pallas kernels, local(): pl.pallas_call(functools.partial(body, dims), out_shape=pltpu.VMEM((1, 2,...  14.3 us
    unnamed x1, local copies, waits for them, and re-layouts  0.66 us

profile of v11, /device:TPU:0, one launch (start us, length us, event | category | flops | bytes accessed | tf_op | source)
XLA Modules:
  0.0 15.0 jit_solution(18308921281645461567)
XLA Ops:
  0.0 14.3 %shard_map.100 = f32[1,2,8,2048]{3,2,1,0:T(8,128)S(1)} custom-call(s32[2,8]{1,0:T(2,128)} %bitcast.3, s32[2,4]{1,0:T(2,128)} %bitcast.4, s32[4,2,4]{2,1,0:T(2,128)} %refs_2_.1, bf16[1,2,8,4096]{3,2,1,0:T(8,128)(2,1)} %refs_3_.1, bf16[1,2,256,256]{3,2,1,0:T(8,128)(2,1)} %refs_4_.1, s32[1,2,1,2,256]{4,3,2,1,0:T(2,128)} %refs_5_.1, ...), custom_call_target="tpu_custom_call" | custom-call | tf_op jit(solution)/shard_map/pallas_call | solution.py:476
  14.3 0.7 %copy.12 = f32[1,2,8,2048]{3,2,1,0:T(8,128)} copy(f32[1,2,8,2048]{3,2,1,0:T(8,128)S(1)} %shard_map.100) | data formatting | bytes 262144

commit v12 on v11

--- a/solution.py
+++ b/solution.py
@@ -76,14 +76,14 @@
     fetches = [
         pltpu.make_async_copy(sub_hbm, sub_off, in_sem.at[0]),
         pltpu.make_async_copy(rows_hbm, rows, in_sem.at[1]),
-        pltpu.make_async_copy(fac_hbm, fac_off, in_sem.at[4]),
+        pltpu.make_async_copy(fac_hbm, fac_off, in_sem.at[0]),
         pltpu.make_async_copy(cnt_hbm, counts, in_sem.at[2]),
         pltpu.make_async_copy(cells_hbm.at[0, my_b, 0], cells, in_sem.at[2]),
         pltpu.make_async_copy(obs_hbm.at[0, my_b, 0], observed, in_sem.at[2]),
         pltpu.make_async_copy(wt_hbm, weights, in_sem.at[2]),
         pltpu.make_async_copy(kt_hbm, kt, in_sem.at[0]),
-        pltpu.make_async_copy(kk_hbm, kk, in_sem.at[1]),
-        pltpu.make_async_copy(aterm_hbm.at[0, my_b], aterm, in_sem.at[3]),
+        pltpu.make_async_copy(kk_hbm, kk, in_sem.at[0]),
+        pltpu.make_async_copy(aterm_hbm.at[0, my_b], aterm, in_sem.at[0]),
     ]
     fetches[0].start()
     fetches[2].start()
@@ -370,12 +370,9 @@
 
     left = [None] * nt
     prod = None
-    for k in range(nt + 1):
-        if k < nt:
-            left[k] = degrid(k)
-        if k:
-            part = mm_nt(left[k - 1], col_w[k - 1])
-            prod = part if prod is None else prod + part
+    for k in range(nt):
+        left[k] = degrid(k)
+    prod = mm_nt(cat(left, 1), cat([col_w[k] for k in range(nt)], 1))
     a, c, b, d = (prod[q * mirror : (q + 1) * mirror] for q in range(4))
     real = cat([a - d, a + d], 0)
     imag = cat([b + c, b - c], 0)
@@ -501,7 +498,7 @@
             vmem((nt, size, slots), BF),
             vmem((nt, size // 2, slots), F32),
             vmem((nt, size // 2, slots), F32),
-            dma, dma, dma((nt,)), dma((3,)), dma((5,)), pltpu.SemaphoreType.REGULAR((max(nt - 1, 1),)),
+            dma, dma, dma((nt,)), dma((3,)), dma((3,)), pltpu.SemaphoreType.REGULAR((max(nt - 1, 1),)),
         ],
         compiler_params=pltpu.CompilerParams(
             collective_id=0, has_side_effects=True

time: 15.2 us -> 15.1 us (level)
  no operation moved by 1% of the time
where the time goes in v12:
time: 15.1 us; the launch traced here: 14.9 us
  Pallas kernels  14.2 us (94%)
  local copies, waits for them, and re-layouts  0.66 us (4%)
    pallas_call x1, Pallas kernels, local(): pl.pallas_call(functools.partial(body, dims), out_shape=pltpu.VMEM((1, 2,...  14.2 us
    unnamed x1, local copies, waits for them, and re-layouts  0.66 us

profile of v12, /device:TPU:0, one launch (start us, length us, event | category | flops | bytes accessed | tf_op | source)
XLA Modules:
  0.0 14.9 jit_solution(14555459606967833694)
XLA Ops:
  0.0 14.2 %shard_map.100 = f32[1,2,8,2048]{3,2,1,0:T(8,128)S(1)} custom-call(s32[2,8]{1,0:T(2,128)} %bitcast.3, s32[2,4]{1,0:T(2,128)} %bitcast.4, s32[4,2,4]{2,1,0:T(2,128)} %refs_2_.1, bf16[1,2,8,4096]{3,2,1,0:T(8,128)(2,1)} %refs_3_.1, bf16[1,2,256,256]{3,2,1,0:T(8,128)(2,1)} %refs_4_.1, s32[1,2,1,2,256]{4,3,2,1,0:T(2,128)} %refs_5_.1, ...), custom_call_target="tpu_custom_call" | custom-call | tf_op jit(solution)/shard_map/pallas_call | solution.py:473
  14.2 0.7 %copy.12 = f32[1,2,8,2048]{3,2,1,0:T(8,128)} copy(f32[1,2,8,2048]{3,2,1,0:T(8,128)S(1)} %shard_map.100) | data formatting | bytes 262144

commit v13 on v12

--- a/solution.py
+++ b/solution.py
@@ -217,7 +217,7 @@
             src_ref=slot_out,
             dst_ref=got_x.at[my_t],
             send_sem=sent,
-            recv_sem=recv_x.at[my_t],
+            recv_sem=recv_x.at[lax.rem(my_t - t + nt, nt) - 1],
             device_id={"facet": my_f, "team": t, "sub": my_b},
             device_id_type=MESH,
         )
@@ -305,7 +305,7 @@
     for k in range(nt):
         src = lax.rem(my_t + k, nt)
         if k:
-            pltpu.make_async_copy(got_x.at[src], got_x.at[src], recv_x.at[src]).wait()
+            pltpu.make_async_copy(got_x.at[src], got_x.at[src], recv_x.at[k - 1]).wait()
         pos = got_x[src].astype(F32)[0:4, :].astype(jnp.int32)
         pos = (pos[0:2, :] << HALF_BITS) + pos[2:4, :]
         pos_x = pos[0:1, :]
@@ -392,7 +392,7 @@
             src_ref=fold_out.at[facet_at(k)],
             dst_ref=got2.at[far, my_f],
             send_sem=sent,
-            recv_sem=recv2.at[min(k // nc, 1) + far],
+            recv_sem=recv2.at[2 + my_c if far and k >= nc else min(k // nc, 1) + far],
             device_id={"facet": facet_at(k), "team": my_t, "sub": other if far else my_b},
             device_id_type=MESH,
         )
@@ -428,8 +428,9 @@
     total = update(total, 1, local_k)
     total = update(total, 0, urgent)
     if ny > 1:
-        arrived(2, nf - nc)
-    total = update(total, 1, urgent)
+        for c in reversed(range(nc)):
+            arrived(2 + c, ny - 1)
+            total = update(total, 1, [k for k in urgent if k % nc == c])
     for k in range(half):
         rng = slice(k * rdev, (k + 1) * rdev)
         lanes = slice(k * LANES, (k + 1) * LANES)
@@ -461,6 +462,7 @@
     slots = cells.shape[-1]
     n = nf * nt
     tiles = length // LANES
+    nc = 2 - nf % 2
     dims = (nf, nt, nb, length, size, rdev)
     consts = [jnp.asarray(v) for v in tables(size)]
     hbm = pl.BlockSpec(memory_space=pltpu.HBM)
@@ -498,7 +500,7 @@
             vmem((nt, size, slots), BF),
             vmem((nt, size // 2, slots), F32),
             vmem((nt, size // 2, slots), F32),
-            dma, dma, dma((nt,)), dma((3,)), dma((3,)), pltpu.SemaphoreType.REGULAR((max(nt - 1, 1),)),
+            dma, dma, dma((max(nt - 1, 1),)), dma((2 + nc,)), dma((3,)), pltpu.SemaphoreType.REGULAR((max(nt - 1, 1),)),
         ],
         compiler_params=pltpu.CompilerParams(
             collective_id=0, has_side_effects=True

time: 15.1 us -> 15 us (level)
  no operation moved by 1% of the time
where the time goes in v13:
time: 15 us; the launch traced here: 14.9 us
  Pallas kernels  14.2 us (95%)
  local copies, waits for them, and re-layouts  0.66 us (4%)
    pallas_call x1, Pallas kernels, local(): pl.pallas_call(functools.partial(body, dims), out_shape=pltpu.VMEM((1, 2,...  14.2 us
    unnamed x1, local copies, waits for them, and re-layouts  0.66 us

profile of v13, /device:TPU:0, one launch (start us, length us, event | category | flops | bytes accessed | tf_op | source)
XLA Modules:
  0.0 14.9 jit_solution(454167586040686219)
XLA Ops:
  0.0 14.2 %shard_map.100 = f32[1,2,8,2048]{3,2,1,0:T(8,128)S(1)} custom-call(s32[2,8]{1,0:T(2,128)} %bitcast.3, s32[2,4]{1,0:T(2,128)} %bitcast.4, s32[4,2,4]{2,1,0:T(2,128)} %refs_2_.1, bf16[1,2,8,4096]{3,2,1,0:T(8,128)(2,1)} %refs_3_.1, bf16[1,2,256,256]{3,2,1,0:T(8,128)(2,1)} %refs_4_.1, s32[1,2,1,2,256]{4,3,2,1,0:T(2,128)} %refs_5_.1, ...), custom_call_target="tpu_custom_call" | custom-call | tf_op jit(solution)/shard_map/pallas_call | solution.py:475
  14.2 0.7 %copy.12 = f32[1,2,8,2048]{3,2,1,0:T(8,128)} copy(f32[1,2,8,2048]{3,2,1,0:T(8,128)S(1)} %shard_map.100) | data formatting | bytes 262144

commit v14 on v13

--- a/solution.py
+++ b/solution.py
@@ -14,7 +14,7 @@
 LANES = 128
 FINE = 16
 HALF_BITS = 5
-PIECES = 2
+PIECES = 1
 TWO_PI = 2.0 * math.pi
 BF = jnp.bfloat16
 F32 = jnp.float32

time: 15 us -> 15 us (level)
  no operation moved by 1% of the time
where the time goes in v14:
time: 15 us; the launch traced here: 14.8 us
  Pallas kernels  14.2 us (95%)
  local copies, waits for them, and re-layouts  0.66 us (4%)
    pallas_call x1, Pallas kernels, local(): pl.pallas_call(functools.partial(body, dims), out_shape=pltpu.VMEM((1, 2,...  14.2 us
    unnamed x1, local copies, waits for them, and re-layouts  0.66 us

profile of v14, /device:TPU:0, one launch (start us, length us, event | category | flops | bytes accessed | tf_op | source)
XLA Modules:
  0.0 14.8 jit_solution(10676517878695969817)
XLA Ops:
  0.0 14.2 %shard_map.100 = f32[1,2,8,2048]{3,2,1,0:T(8,128)S(1)} custom-call(s32[2,8]{1,0:T(2,128)} %bitcast.3, s32[2,4]{1,0:T(2,128)} %bitcast.4, s32[4,2,4]{2,1,0:T(2,128)} %refs_2_.1, bf16[1,2,8,4096]{3,2,1,0:T(8,128)(2,1)} %refs_3_.1, bf16[1,2,256,256]{3,2,1,0:T(8,128)(2,1)} %refs_4_.1, s32[1,2,1,2,256]{4,3,2,1,0:T(2,128)} %refs_5_.1, ...), custom_call_target="tpu_custom_call" | custom-call | tf_op jit(solution)/shard_map/pallas_call | solution.py:475
  14.2 0.7 %copy.12 = f32[1,2,8,2048]{3,2,1,0:T(8,128)} copy(f32[1,2,8,2048]{3,2,1,0:T(8,128)S(1)} %shard_map.100) | data formatting | bytes 262144
